TPU v7x, 256 devices: a whole 4x4x8 slice. The times are simulated.
256 devices in a mesh: seq: 32 (over y, z), ch: 8 (over x, core).
Axes of the slice: x: 4, y: 4, z: 8, core: 2. Of those that a mesh axis runs over, the one named last changes fastest.
Arguments:
- tokens: bfloat16 [4096, 4096], P('seq', 'ch'), may hold values from -6 to 6
- norm_gain: float32 [4096], replicated, may hold values from 0.5 to 1.5
- in_proj: bfloat16 [4096, 2, 8192], P('seq', None, 'ch'), may hold values from -0.09375 to 0.09375
- conv_weight: float32 [4, 8192], P(None, 'ch'), may hold values from -3 to 3
- conv_bias: float32 [8192], P('ch'), may hold values from -2 to 2
- x_proj: bfloat16 [8192, 544], P('ch'), may hold values from -0.0625 to 0.0625
- dt_proj: bfloat16 [512, 8192], P(None, 'ch'), may hold values from -0.25 to 0.25
- dt_bias: float32 [8192], P('ch'), may hold values from -4 to 1
- a_log: float32 [8192, 16], P('ch'), as said below
- d_skip: float32 [8192], P('ch'), may hold values from -32 to 32
- out_proj: bfloat16 [8192, 4096], P('ch', 'seq'), may hold values from -0.0625 to 0.0625
Outputs:
- mixed: bfloat16 [4096, 4096], P('seq', 'ch')
Inputs may be any that keep to these rules, and one draw needn't show every extreme that they name: Every entry of a_log lies between ln(0.2 / 4096) and ln(0.2).
All inputs are finite; a program needn't handle non-finite values.
Results may differ from a plain program's by a relative error of at most 0.014.
Values may be sent and summed in bfloat16 or wider, within the bound.
No kernel may reach another device: no remote copies, remote signals or barrier semaphores. Data moves between devices by JAX's collectives and lax.ppermute only.
A program may use at most 64 MiB of HBM per device.

v0:
```python
import functools

import jax
import jax.numpy as jnp
from jax import lax
from jax.experimental import pallas as pl
from jax.experimental.pallas import tpu as pltpu
from jax.sharding import Mesh
from jax.sharding import PartitionSpec as P


SEQ = ("y", "z")
CH = ("x", "c")
HALO = 16
AXES = ("y", "z", "x", "c")
Y, Z, X, C = range(4)
LOG2E = 1.4426950408889634


def shifted(block, axis, distance):
    n = lax.axis_size(axis)
    return lax.ppermute(block, axis, [(i, (i + distance) % n) for i in range(n)])


def from_behind(block, axis):
    return [block] + [shifted(block, axis, k) for k in range(1, lax.axis_size(axis))]


def given_back(pieces, axis):
    return [pieces[0]] + [shifted(pieces[k], axis, -k) for k in range(1, len(pieces))]


def place():
    return jnp.stack([lax.axis_index(axis) for axis in AXES]).astype(jnp.int32)


def call(kernel, out_shape, *operands, scratch=()):
    whole = pl.BlockSpec(memory_space=pltpu.VMEM)
    return pl.pallas_call(
        kernel,
        out_shape=out_shape,
        in_specs=[pl.BlockSpec(memory_space=pltpu.SMEM)] + [whole] * (len(operands) - 1),
        out_specs=jax.tree.map(lambda _: whole, out_shape),
        scratch_shapes=scratch,
    )(*operands)


def array(shape, dtype=jnp.float32):
    return jax.ShapeDtypeStruct(shape, dtype)


def project_pieces(n, place_ref, zero, one, w_ref):
    width = zero[0].shape[1]
    rows = zero[0].shape[0] // n
    left = [
        jnp.concatenate([ref[...] for ref in zero], 1),
        jnp.concatenate(
            [
                jnp.concatenate([ref[k * rows : (k + 1) * rows] for k in range(n)], 1)
                for ref in one
            ],
            0,
        ),
    ]
    total = None
    for c in range(2):
        weights = []
        for k in range(n):
            x = lax.rem(place_ref[X] + n - k, n)
            for q in range(width // 128):
                start = pl.multiple_of(((c * (width // 128) + q) * n + x) * 128, 128)
                weights.append(w_ref[pl.ds(start, 128), :])
        weight = jnp.concatenate(weights, 0)
        product = jnp.dot(left[c], weight, preferred_element_type=jnp.float32)
        total = product if total is None else total + product
    return left, total


def conv_project_kernel(n, features, place_ref, *refs):
    pieces, w_ref, out_ref, scale_ref = refs[: 2 * n], refs[2 * n], refs[-2], refs[-1]

    def finish(zero, one):
        left, total = project_pieces(n, place_ref, zero, one, w_ref)
        rows = total.shape[0] // n
        for k in range(n):
            where = slice(k * rows, (k + 1) * rows)
            square = jnp.zeros((rows, 128), jnp.float32)
            for side in left:
                for f in range(side.shape[1] // 128):
                    wide = side[where, f * 128 : (f + 1) * 128].astype(jnp.float32)
                    square = square + wide * wide
            square = jnp.sum(square, axis=-1, keepdims=True)
            scale = lax.rsqrt(square * (1.0 / features) + 1e-06)
            scale_ref[where, :] = jnp.broadcast_to(scale, (rows, 128))
            block = total[where] * scale
            out_ref[lax.rem(place_ref[Y] + n - k, n)] = block.astype(jnp.bfloat16)

    pl.when(place_ref[C] == 0)(lambda: finish(pieces[:n], pieces[n:]))
    pl.when(place_ref[C] == 1)(lambda: finish(pieces[n:], pieces[:n]))


def gate_project_kernel(n, place_ref, *refs):
    pieces, w_ref, scale_ref, outs = refs[: 2 * n], refs[2 * n], refs[2 * n + 1], refs[2 * n + 2 :]

    def finish(zero, one):
        _, total = project_pieces(n, place_ref, zero, one, w_ref)
        rows = total.shape[0] // n
        for k in range(n):
            where = slice(k * rows + HALO, (k + 1) * rows)
            scale = scale_ref[where, :1]
            outs[k][...] = (total[where] * scale).astype(jnp.bfloat16)

    pl.when(place_ref[C] == 0)(lambda: finish(pieces[:n], pieces[n:]))
    pl.when(place_ref[C] == 1)(lambda: finish(pieces[n:], pieces[:n]))


def conv_kernel(place_ref, got_ref, w_ref, bias_ref, proj_ref, act_ref, kept_ref, given_ref, whole_ref):
    n, rows, width = got_ref.shape
    tokens = rows - HALO
    per = width // 128
    total = None
    for q in range(n):
        lanes = slice(q * width, (q + 1) * width)
        wide = got_ref[q].astype(jnp.float32)
        mixed = bias_ref[:, lanes]
        for tap in range(4):
            first = HALO - 3 + tap
            mixed = mixed + w_ref[tap : tap + 1, lanes] * wide[first : first + tokens]
        active = mixed * jax.nn.sigmoid(mixed)
        for h in range(per):
            for t in range(tokens // 8):
                row = (t * n * per + q * per + h) * 8
                act_ref[row : row + 8, :] = active[t * 8 : t * 8 + 8, h * 128 : h * 128 + 128]
        product = lax.dot_general(
            active.astype(jnp.bfloat16),
            proj_ref[:, lanes],
            (((1,), (1,)), ((), ())),
            preferred_element_type=jnp.float32,
        )
        total = product if total is None else total + product
    whole_ref[...] = total
    half = tokens // 2
    mine = place_ref[C]
    kept_ref[...] = whole_ref[pl.ds(pl.multiple_of(mine * half, half), half), :]
    given_ref[...] = whole_ref[pl.ds(pl.multiple_of((1 - mine) * half, half), half), :]


def joined_halves(place_ref, mine_ref, theirs_ref, all_ref):
    half = mine_ref.shape[0]
    mine = place_ref[C]
    all_ref[pl.ds(pl.multiple_of(mine * half, half), half), :] = mine_ref[...]
    all_ref[pl.ds(pl.multiple_of((1 - mine) * half, half), half), :] = theirs_ref[...]


def spread(all_ref, first, states, out_ref):
    tokens = all_ref.shape[0]
    tail = all_ref[:, first : first + states]
    for n in range(states):
        column = jnp.broadcast_to(tail[:, n : n + 1], (tokens, 128))
        out_ref[n * tokens : (n + 1) * tokens, :] = column


def scan_loop(tokens, states, begin, step_ref, act_ref, a_ref, b_ref, c_ref=None, emit=None):
    rates = [a_ref[n] for n in range(states)]

    def eight_tokens(tile, carry):
        state, steps = list(carry[0]), carry[1]
        for s in range(8):
            rows = pl.ds(tile * 64 + s, 8, stride=8)
            step, active = step_ref[rows, :], act_ref[rows, :]
            drive = step * active
            total = None
            for n in range(states):
                row = pl.ds(n * tokens + tile * 8 + s, 1)
                decay = jnp.exp2(step * rates[n])
                state[n] = decay * state[n] + drive * b_ref[row, :]
                if emit is not None:
                    part = state[n] * c_ref[row, :]
                    total = part if total is None else total + part
            if emit is not None:
                emit(rows, total, active)
            else:
                steps = steps + step
        return tuple(state), steps

    return lax.fori_loop(0, tokens // 8, eight_tokens, (begin, jnp.zeros((8, 128), jnp.float32)))


def store_packed(out_ref, steps, state):
    high = steps.astype(jnp.bfloat16)
    low = (steps - high.astype(jnp.float32)).astype(jnp.bfloat16)
    for copy in range(out_ref.shape[0]):
        out_ref[copy, 0] = high
        out_ref[copy, 1] = low
        for n, value in enumerate(state):
            out_ref[copy, 2 + n] = value.astype(jnp.bfloat16)


def steps_of(got_ref, k):
    return got_ref[k, 0].astype(jnp.float32) + got_ref[k, 1].astype(jnp.float32)


def prescan_kernel(
    place_ref, mine_ref, theirs_ref, dt_ref, bias_ref, act_ref, a_ref, step_ref, end_ref, all_ref, b_ref
):
    joined_halves(place_ref, mine_ref, theirs_ref, all_ref)
    tokens = all_ref.shape[0]
    rank, channels = dt_ref.shape
    states = a_ref.shape[0]
    spread(all_ref, rank, states, b_ref)
    raw = all_ref[:, :rank].astype(jnp.bfloat16)
    value = jnp.dot(raw, dt_ref[...], preferred_element_type=jnp.float32) + bias_ref[...]
    value = jnp.maximum(value, 0.0) + jnp.log1p(jnp.exp(-jnp.abs(value)))
    for t in range(tokens // 8):
        for j in range(channels // 128):
            row = (t * (channels // 128) + j) * 8
            step_ref[row : row + 8, :] = value[t * 8 : t * 8 + 8, j * 128 : j * 128 + 128]
    begin = tuple(jnp.zeros((8, 128), jnp.float32) for _ in range(states))
    final, steps = scan_loop(tokens, states, begin, step_ref, act_ref, a_ref, b_ref)
    store_packed(end_ref, steps, final)


def row_kernel(place_ref, got_ref, a_ref, inside_ref, whole_ref):
    states = a_ref.shape[0]
    zero = jnp.zeros(a_ref.shape[1:], jnp.float32)
    steps, state = zero, [zero] * states
    for k in range(got_ref.shape[0]):

        @pl.when(place_ref[Z] == k)
        def _(steps=steps, state=tuple(state)):
            for n in range(states):
                inside_ref[n] = state[n]
            inside_ref[states] = steps

        own = steps_of(got_ref, k)
        for n in range(states):
            end = got_ref[k, 2 + n].astype(jnp.float32)
            state[n] = jnp.exp2(a_ref[n] * own) * state[n] + end
        steps = steps + own
    store_packed(whole_ref, steps, state)


def rescan_kernel(n, place_ref, mine_ref, theirs_ref, step_ref, act_ref, a_ref, far_ref, near_ref, skip_ref, *refs):
    gates, out_ref = refs[:n], refs[n]
    all_ref, b_ref, c_ref, y_ref = refs[n + 1 :]
    joined_halves(place_ref, mine_ref, theirs_ref, all_ref)
    tokens, width = gates[0].shape
    states = a_ref.shape[0]
    first = all_ref.shape[1] - 2 * states
    spread(all_ref, first, states, b_ref)
    spread(all_ref, first + states, states, c_ref)
    skip = skip_ref[...]
    since = near_ref[states]
    begin = [jnp.zeros_like(since)] * states
    for k in range(far_ref.shape[0] - 1):
        before = k < place_ref[Y]
        own = steps_of(far_ref, k)
        for i in range(states):
            row = jnp.exp2(a_ref[i] * own) * begin[i] + far_ref[k, 2 + i].astype(jnp.float32)
            begin[i] = jnp.where(before, row, begin[i])
    begin = tuple(jnp.exp2(a_ref[i] * since) * begin[i] + near_ref[i] for i in range(states))

    def emit(rows, total, active):
        y_ref[rows, :] = total + skip * active

    scan_loop(tokens, states, begin, step_ref, act_ref, a_ref, b_ref, c_ref, emit)
    per = width // 128
    for k in range(n):
        q = lax.rem(place_ref[Y] + k, n)
        for h in range(per):
            gate = gates[k][:, h * 128 : h * 128 + 128].astype(jnp.float32)
            parts = []
            for t in range(tokens // 8):
                row = pl.multiple_of((t * n * per + q * per + h) * 8, 8)
                parts.append(y_ref[pl.ds(row, 8), :])
            value = jnp.concatenate(parts, 0) * (gate * jax.nn.sigmoid(gate))
            lanes = pl.ds(pl.multiple_of((q * per + h) * 128, 128), 128)
            out_ref[:, lanes] = value.astype(jnp.bfloat16)


def output_kernel(n, place_ref, *refs):
    pieces, w_ref, given_ref, kept_ref = refs[:n], refs[n], refs[n + 1], refs[n + 2]
    half = w_ref.shape[1] // 2
    rows = pieces[0].shape[0]
    left = jnp.concatenate([ref[...] for ref in pieces], 0)
    for out_ref, h in ((given_ref, 1 - place_ref[C]), (kept_ref, place_ref[C])):
        lanes = pl.ds(pl.multiple_of(h * half, half), half)
        product = jnp.dot(left, w_ref[:, lanes], preferred_element_type=jnp.float32)
        product = product.astype(jnp.bfloat16)
        for r in range(n):
            out_ref[r] = product[r * rows : (r + 1) * rows]


def pair_kernel(n, place_ref, kept_ref, got_ref, *outs):
    for k in range(n):
        r = lax.rem(place_ref[X] + 2 * n - place_ref[Y] - k, n)
        pair = kept_ref[r].astype(jnp.float32) + got_ref[r].astype(jnp.float32)
        outs[k][...] = pair.astype(jnp.bfloat16)


def spread_tokens(tokens):
    n = lax.axis_size("y")
    order = [(i, i + 1) for i in range(lax.axis_size(SEQ) - 1)]
    ahead = lax.ppermute(tokens[-HALO:], SEQ, order)
    block = jnp.concatenate([ahead, tokens], 0)
    for stage in range(2):
        got = [block]
        for k in range(1, n):
            route = []
            for y in range(n):
                for x in range(n):
                    for c in range(2):
                        to = ((y + k) % n, x) if c == stage else (y, (x + k) % n)
                        route.append(((y * n + x) * 2 + c, (to[0] * n + to[1]) * 2 + c))
            got.append(lax.ppermute(block, ("y", "x", "c"), route))
        block = jnp.concatenate(got, 0) if stage == 0 else got
    return block


def on_device(
    tokens,
    norm_gain,
    in_proj,
    conv_weight,
    conv_bias,
    x_proj,
    dt_proj,
    dt_bias,
    a_log,
    d_skip,
    out_proj,
):
    local_tokens = tokens.shape[0]
    channels = in_proj.shape[2]
    n = lax.axis_size("y")
    states = a_log.shape[1]
    features_out = x_proj.shape[1]
    tile_rows = local_tokens * channels // 128
    width = channels // n
    where = place()

    features = norm_gain.shape[0]
    count = in_proj.shape[0]
    gain = lax.dynamic_slice_in_dim(norm_gain, lax.axis_index(SEQ) * count, count, 0)
    gained = (in_proj.astype(jnp.float32) * gain[:, None, None]).astype(jnp.bfloat16)
    quarters = gained.reshape(-1, 2, n, width).transpose(2, 1, 0, 3)
    quarters = lax.all_to_all(quarters, "y", 0, 0, tiled=True)
    conv_w = lax.all_gather(quarters[:, 0].reshape(-1, width), "z", axis=0, tiled=True)
    gate_w = lax.all_gather(quarters[:, 1].reshape(-1, width), "z", axis=0, tiled=True)

    own = spread_tokens(tokens)
    pieces = own + [shifted(own[0], "c", 1)]
    pieces += [shifted(piece, "c", 1) for piece in own[1:]]
    rows = own[0].shape[0]
    conv_quad, scale = call(
        functools.partial(conv_project_kernel, n, features),
        (array((n, rows // n, width), jnp.bfloat16), array((rows, 128))),
        where,
        *pieces,
        conv_w,
    )
    conv_got = lax.all_to_all(conv_quad, "y", 0, 0, tiled=True)
    act_tiles, kept, given = call(
        conv_kernel,
        (
            array((tile_rows, 128)),
            array((local_tokens // 2, features_out)),
            array((local_tokens // 2, features_out)),
        ),
        where,
        conv_got,
        conv_weight,
        conv_bias.reshape(1, -1),
        x_proj.T,
        scratch=[pltpu.VMEM((local_tokens, features_out), jnp.float32)],
    )
    pair = kept + shifted(given, "c", 1)
    behind = from_behind(pair, "x")
    mine = sum(behind[1:], pair)
    theirs = shifted(mine, "c", 1)

    swap = [(y * n + x, x * n + y) for y in range(n) for x in range(n)]
    turned = lax.ppermute(out_proj, ("y", "x"), swap)
    out_w = lax.all_gather(turned, "z", axis=1, tiled=True)

    gate_quad = call(
        functools.partial(gate_project_kernel, n),
        tuple(array((local_tokens, width), jnp.bfloat16) for _ in range(n)),
        where,
        *pieces,
        gate_w,
        scale,
    )
    gate_got = given_back(gate_quad, "y")

    rates = (-LOG2E * jnp.exp(a_log)).T.reshape(states, channels // 128, 128)
    shard = (states + 2, *rates.shape[1:])
    all_features = pltpu.VMEM((local_tokens, features_out), jnp.float32)
    spread_rows = pltpu.VMEM((local_tokens * states, 128), jnp.float32)
    step_tiles, packed = call(
        prescan_kernel,
        (array((tile_rows, 128)), array((lax.axis_size("z"), *shard), jnp.bfloat16)),
        where,
        mine,
        theirs,
        dt_proj,
        dt_bias.reshape(1, -1),
        act_tiles,
        rates,
        scratch=[all_features, spread_rows],
    )
    ends = lax.all_to_all(packed, "z", 0, 0, tiled=True)
    near, whole = call(
        row_kernel,
        (array((states + 1, *rates.shape[1:])), array((n, *shard), jnp.bfloat16)),
        where,
        ends,
        rates,
    )
    far = lax.all_to_all(whole, "y", 0, 0, tiled=True)
    gated = call(
        functools.partial(rescan_kernel, n),
        array((local_tokens, channels), jnp.bfloat16),
        where,
        mine,
        theirs,
        step_tiles,
        act_tiles,
        rates,
        far,
        near,
        d_skip.reshape(channels // 128, 128),
        *gate_got,
        scratch=[all_features, spread_rows, spread_rows, pltpu.VMEM((tile_rows, 128), jnp.float32)],
    )

    held = [
        lax.ppermute(
            gated,
            ("y", "x"),
            [(y * n + x, x * n + (y + r) % n) for y in range(n) for x in range(n)],
        )
        for r in range(n)
    ]
    half = array((n, local_tokens, out_w.shape[1] // 2), jnp.bfloat16)
    given, kept = call(functools.partial(output_kernel, n), (half, half), where, *held, out_w)
    sent = call(
        functools.partial(pair_kernel, n),
        tuple(array(half.shape[1:], jnp.bfloat16) for _ in range(n)),
        where,
        kept,
        shifted(given, "c", 1),
    )
    arrived = [sent[0]] + [shifted(sent[k], "y", k) for k in range(1, n)]
    mixed = sum((piece.astype(jnp.float32) for piece in arrived[1:]), arrived[0].astype(jnp.float32))
    return mixed.astype(jnp.bfloat16)


def solution(mesh):
    torus = Mesh(mesh.devices.reshape(4, 8, 4, 2), ("y", "z", "x", "c"))
    return jax.shard_map(
        on_device,
        mesh=torus,
        in_specs=(
            P(SEQ, CH),
            P(),
            P(SEQ, None, CH),
            P(None, CH),
            P(CH),
            P(CH, None),
            P(None, CH),
            P(CH),
            P(CH, None),
            P(CH),
            P(CH, SEQ),
        ),
        out_specs=P(SEQ, CH),
        check_vma=False,
    )
```

profile of v0, /device:TPU:1, one launch (start us, length us, event | category | flops | bytes accessed | tf_op | source)
XLA Modules:
  0.0 215.6 jit_solution(8234539785750566250)
XLA Ops:
  6.5 1.4 copy.13
  9.0 13.4 %all_to_all.20 = bf16[4,2,128,256]{3,2,1,0:T(8,128)(2,1)S(1)} all-to-all(bf16[4,2,128,256]{3,2,1,0:T(8,128)(2,1)S(1)} %copy.14), channel_id=1, replica_groups=mesh['y'=4,'z'=8,'x'=4,'c'=2] {'y'}, dimensions={0} | all-to-all | bytes 1048576 | tf_op jit(solution)/shard_map/all_to_all | solution.py:347
  22.5 0.8 fusion
  24.8 3.5 %collective-permute-start = (bf16[16,512]{1,0:T(8,128)(2,1)S(1)}, bf16[16,512]{1,0:T(8,128)(2,1)S(1)}, u32[]{:S(2)}, u32[]{:S(2)}) collective-permute-start(bf16[16,512]{1,0:T(8,128)(2,1)S(1)} %slice.9), channel_id=1, source_target_pairs={{0,8},{8,16},{16,24},{24,32},{32,40},{40,48},{48,56},{56,64},{64,7... | collective-permute-start | bytes 49160 | tf_op jit(solution)/shard_map/ppermute | solution.py:304
  29.3 7.5 %collective-permute-start.1 = (bf16[144,512]{1,0:T(8,128)(2,1)S(1)}, bf16[144,512]{1,0:T(8,128)(2,1)S(1)}, u32[]{:S(2)}, u32[]{:S(2)}) collective-permute-start(bf16[144,512]{1,0:T(8,128)(2,1)S(1)} %get-tuple-element.45), channel_id=1, source_target_pairs={{0,64},{1,3},{2,66},{3,5},{4,68},{5,7},{6,70},{7,1},{64,128},{65,6... | collective-permute-start | bytes 442376 | tf_op jit(solution)/shard_map/ppermute | solution.py:315
  36.8 10.6 %collective-permute-start.2 = (bf16[144,512]{1,0:T(8,128)(2,1)S(1)}, bf16[144,512]{1,0:T(8,128)(2,1)S(1)}, u32[]{:S(2)}, u32[]{:S(2)}) collective-permute-start(bf16[144,512]{1,0:T(8,128)(2,1)S(1)} %get-tuple-element.45), channel_id=1, source_target_pairs={{0,128},{1,5},{2,130},{3,7},{4,132},{5,1},{6,134},{7,3},{64,192},{... | collective-permute-start | bytes 442376 | tf_op jit(solution)/shard_map/ppermute | solution.py:315
  47.4 1.7 collective-permute-done.1
  49.2 2.4 %collective-permute-done.2 = bf16[144,512]{1,0:T(8,128)(2,1)S(1)} collective-permute-done((bf16[144,512]{1,0:T(8,128)(2,1)S(1)}, bf16[144,512]{1,0:T(8,128)(2,1)S(1)}, u32[]{:S(2)}, u32[]{:S(2)}) %collective-permute-start.2) | collective-permute-done | bytes 147488 | tf_op jit(solution)/shard_map/ppermute | solution.py:315
  52.4 0.9 collective-permute-start.4
  53.7 4.1 %collective-permute-start.7 = (bf16[576,512]{1,0:T(8,128)(2,1)S(1)}, bf16[576,512]{1,0:T(8,128)(2,1)S(1)}, u32[]{:S(2)}, u32[]{:S(2)}) collective-permute-start(bf16[576,512]{1,0:T(8,128)(2,1)S(1)} %constant_dynamic-update-slice_fusion.2.refs_0_), channel_id=1, source_target_pairs={{0,1},{1,0},{2,3},{3,2},{4,5},{5,4},{6,7},{7,6},{8,9},{9,8},{10,11... | collective-permute-start | bytes 1769480 | tf_op jit(solution)/shard_map/ppermute | solution.py:22
  57.8 3.1 %collective-permute-done.6.refs_3_ = bf16[576,512]{1,0:T(8,128)(2,1)S(1)} collective-permute-done((bf16[576,512]{1,0:T(8,128)(2,1)S(1)}, bf16[576,512]{1,0:T(8,128)(2,1)S(1)}, u32[]{:S(2)}, u32[]{:S(2)}) %collective-permute-start.6) | collective-permute-done | bytes 589856 | tf_op jit(solution)/shard_map/ppermute | solution.py:315
  60.9 9.0 %collective-permute-start.10 = (bf16[576,512]{1,0:T(8,128)(2,1)S(1)}, bf16[576,512]{1,0:T(8,128)(2,1)S(1)}, u32[]{:S(2)}, u32[]{:S(2)}) collective-permute-start(bf16[576,512]{1,0:T(8,128)(2,1)S(1)} %collective-permute-done.6.refs_3_), channel_id=1, source_target_pairs={{0,1},{1,0},{2,3},{3,2},{4,5},{5,4},{6,7},{7,6},{8,9},{9,8},{10,11... | collective-permute-start | bytes 1769480 | tf_op jit(solution)/shard_map/ppermute | solution.py:22
  70.0 3.7 %collective-permute-start.8 = (bf16[576,512]{1,0:T(8,128)(2,1)S(1)}, bf16[576,512]{1,0:T(8,128)(2,1)}, u32[]{:S(2)}, u32[]{:S(2)}) collective-permute-start(bf16[576,512]{1,0:T(8,128)(2,1)S(1)} %collective-permute-done.4.refs_1_), channel_id=1, source_target_pairs={{0,1},{1,0},{2,3},{3,2},{4,5},{5,4},{6,7},{7,6},{8,9},{9,8},{10,11... | collective-permute-start | bytes 1769480 | tf_op jit(solution)/shard_map/ppermute | solution.py:22
  74.4 1.0 collective-permute-done.8.refs_5_
  75.4 0.8 collective-permute-done.9.refs_6_
  76.3 5.4 %shard_map.109 = (bf16[4,144,256]{2,1,0:T(8,128)(2,1)}, f32[576,128]{1,0:T(8,128)}) custom-call(s32[4]{0:T(128)} %pad_add_fusion.place_ref, bf16[576,512]{1,0:T(8,128)(2,1)} %copy-done, bf16[576,512]{1,0:T(8,128)(2,1)} %copy-done.2, bf16[576,512]{1,0:T(8,128)(2,1)} %copy-done.3, bf16[576,512]{1,0:T(8,128)(2,1)} %copy-done.1, bf16[576,512]{1,0:T(8,128)(2,1)} %copy-done.4, ...), custom_call_target="tpu_custom_call" | custom-call | tf_op jit(solution)/shard_map/pallas_call | solution.py:39
  81.7 10.9 %all_to_all.21.got_ref = bf16[4,144,256]{2,1,0:T(8,128)(2,1)} all-to-all(bf16[4,144,256]{2,1,0:T(8,128)(2,1)} %get-tuple-element.24), channel_id=1, replica_groups=mesh['y'=4,'z'=8,'x'=4,'c'=2] {'y'}, dimensions={0} | all-to-all | bytes 589824 | tf_op jit(solution)/shard_map/all_to_all | solution.py:362
  92.7 2.8 %shard_map.110 = (f32[1024,128]{1,0:T(8,128)}, f32[64,544]{1,0:T(8,128)}, f32[64,544]{1,0:T(8,128)}) custom-call(s32[4]{0:T(128)} %pad_add_fusion.place_ref, bf16[4,144,256]{2,1,0:T(8,128)(2,1)} %all_to_all.21.got_ref, f32[4,1024]{1,0:T(4,128)} %w_ref.1, f32[1,1024]{1,0:T(1,128)} %bitcast.24, bf16[544,1024]{1,0:T(8,128)(2,1)} %bitcast.18), custom_call_target="tpu_custom_call" | custom-call | tf_op jit(solution)/shard_map/pallas_call | solution.py:39
  95.5 1.3 collective-permute-start.11
  96.8 1.2 collective-permute-done.11
  98.1 0.9 add.29
  99.3 1.7 collective-permute-start.13
  101.0 1.0 collective-permute-start.14
  102.0 7.4 %collective-permute-done.12 = f32[64,544]{1,0:T(8,128)S(1)} collective-permute-done((f32[64,544]{1,0:T(8,128)S(1)}, f32[64,544]{1,0:T(8,128)S(1)}, u32[]{:S(2)}, u32[]{:S(2)}) %collective-permute-start.12) | collective-permute-done | bytes 139296 | tf_op jit(solution)/shard_map/ppermute | solution.py:22
  109.8 1.6 collective-permute-start.15
  113.0 4.5 %shard_map.111 = (f32[1024,128]{1,0:T(8,128)}, bf16[8,18,8,128]{3,2,1,0:T(8,128)(2,1)}) custom-call(s32[4]{0:T(128)} %pad_add_fusion.place_ref, f32[64,544]{1,0:T(8,128)} %copy-done.6, f32[64,544]{1,0:T(8,128)} %copy-done.7, bf16[512,1024]{1,0:T(8,128)(2,1)} %dt_ref.1, f32[1,1024]{1,0:T(1,128)} %bitcast.25, f32[1024,128]{1,0:T(8,128)} %get-tuple-element.27.act_ref, ...), custom_call_target="tpu_custom_call" | custom-call | tf_op jit(solution)/shard_map/pallas_call | solution.py:39
  117.6 22.7 %all_to_all.22.got_ref = bf16[8,18,8,128]{3,2,1,0:T(8,128)(2,1)} all-to-all(bf16[8,18,8,128]{3,2,1,0:T(8,128)(2,1)} %get-tuple-element.29), channel_id=1, replica_groups=mesh['y'=4,'z'=8,'x'=4,'c'=2] {'z'}, dimensions={0} | all-to-all | bytes 589824 | tf_op jit(solution)/shard_map/all_to_all | solution.py:412
  140.3 1.8 shard_map.112
  142.1 3.3 %all-to-all-start.3 = ((bf16[4,18,8,128]{3,2,1,0:T(8,128)(2,1)}), bf16[4,18,8,128]{3,2,1,0:T(8,128)(2,1)S(1)}, u32[]{:S(2)}, u32[]{:S(2)}) async-start(bf16[4,18,8,128]{3,2,1,0:T(8,128)(2,1)} %get-tuple-element.30), calls=%async_computation.3 | async-start | bytes 294912 | tf_op jit(solution)/shard_map/all_to_all | solution.py:420
  145.5 5.2 %shard_map.113 = (bf16[128,256]{1,0:T(8,128)(2,1)}, bf16[128,256]{1,0:T(8,128)(2,1)}, bf16[128,256]{1,0:T(8,128)(2,1)}, bf16[128,256]{1,0:T(8,128)(2,1)}) custom-call(s32[4]{0:T(128)} %pad_add_fusion.place_ref, bf16[576,512]{1,0:T(8,128)(2,1)} %copy-done, bf16[576,512]{1,0:T(8,128)(2,1)} %copy-done.2, bf16[576,512]{1,0:T(8,128)(2,1)} %copy-done.3, ...), custom_call_target="tpu_custom_call" | custom-call | tf_op jit(solution)/shard_map/pallas_call | solution.py:39
  150.7 2.6 %collective-permute-start.16 = (bf16[128,256]{1,0:T(8,128)(2,1)}, bf16[128,256]{1,0:T(8,128)(2,1)S(1)}, u32[]{:S(2)}, u32[]{:S(2)}) collective-permute-start(bf16[128,256]{1,0:T(8,128)(2,1)} %get-tuple-element.34), channel_id=1, source_target_pairs={{0,192},{64,0},{128,64},{192,128},{1,193},{65,1},{129,65},{193,129... | collective-permute-start | bytes 196616 | tf_op jit(solution)/shard_map/ppermute | solution.py:22
  154.9 3.2 %collective-permute-done.17.refs_2_ = bf16[128,256]{1,0:T(8,128)(2,1)S(1)} collective-permute-done((bf16[128,256]{1,0:T(8,128)(2,1)}, bf16[128,256]{1,0:T(8,128)(2,1)S(1)}, u32[]{:S(2)}, u32[]{:S(2)}) %collective-permute-start.17) | collective-permute-done | bytes 65568 | tf_op jit(solution)/shard_map/ppermute | solution.py:22
  158.2 1.1 collective-permute-done.18.refs_3_
  159.9 5.2 %shard_map.114 = bf16[128,1024]{1,0:T(8,128)(2,1)} custom-call(s32[4]{0:T(128)} %pad_add_fusion.place_ref, f32[64,544]{1,0:T(8,128)} %copy-done.6, f32[64,544]{1,0:T(8,128)} %copy-done.7, f32[1024,128]{1,0:T(8,128)} %get-tuple-element.28.step_ref, f32[1024,128]{1,0:T(8,128)} %get-tuple-element.27.act_ref, f32[16,8,128]{2,1,0:T(8,128)} %bitcast.21, ...), custom_call_target="tpu_custom_call" | custom-call | tf_op jit(solution)/shard_map/pallas_call | solution.py:39
  165.1 1.6 collective-permute-start.19
  166.7 1.0 collective-permute-start.20
  167.8 2.9 %collective-permute-start.21 = (bf16[128,1024]{1,0:T(8,128)(2,1)}, bf16[128,1024]{1,0:T(8,128)(2,1)S(1)}, u32[]{:S(2)}, u32[]{:S(2)}) collective-permute-start(bf16[128,1024]{1,0:T(8,128)(2,1)} %shard_map.114), channel_id=1, source_target_pairs={{0,4},{2,68},{4,132},{6,196},{64,6},{66,70},{68,134},{70,198},{128... | collective-permute-start | bytes 786440 | tf_op jit(solution)/shard_map/ppermute | solution.py:438
  170.7 3.7 %collective-permute-start.22 = (bf16[128,1024]{1,0:T(8,128)(2,1)}, bf16[128,1024]{1,0:T(8,128)(2,1)S(1)}, u32[]{:S(2)}, u32[]{:S(2)}) collective-permute-start(bf16[128,1024]{1,0:T(8,128)(2,1)} %shard_map.114), channel_id=1, source_target_pairs={{0,6},{2,70},{4,134},{6,198},{64,0},{66,64},{68,128},{70,192},{128... | collective-permute-start | bytes 786440 | tf_op jit(solution)/shard_map/ppermute | solution.py:438
  174.4 10.3 %collective-permute-done.20.refs_1_ = bf16[128,1024]{1,0:T(8,128)(2,1)S(1)} collective-permute-done((bf16[128,1024]{1,0:T(8,128)(2,1)}, bf16[128,1024]{1,0:T(8,128)(2,1)S(1)}, u32[]{:S(2)}, u32[]{:S(2)}) %collective-permute-start.20) | collective-permute-done | bytes 262176 | tf_op jit(solution)/shard_map/ppermute | solution.py:438
  186.2 4.0 %shard_map.115 = (bf16[4,128,512]{2,1,0:T(8,128)(2,1)}, bf16[4,128,512]{2,1,0:T(8,128)(2,1)}) custom-call(s32[4]{0:T(128)} %pad_add_fusion.place_ref, bf16[128,1024]{1,0:T(8,128)(2,1)} %copy-done.11, bf16[128,1024]{1,0:T(8,128)(2,1)} %copy-done.12, bf16[128,1024]{1,0:T(8,128)(2,1)} %copy-done.13, bf16[128,1024]{1,0:T(8,128)(2,1)} %copy-done.14, ...), custom_call_target="tpu_custom_call" | custom-call | tf_op jit(solution)/shard_map/pallas_call | solution.py:39
  190.2 3.1 %collective-permute-start.24 = (bf16[4,128,512]{2,1,0:T(8,128)(2,1)}, bf16[4,128,512]{2,1,0:T(8,128)(2,1)S(1)}, u32[]{:S(2)}, u32[]{:S(2)}) collective-permute-start(bf16[4,128,512]{2,1,0:T(8,128)(2,1)} %get-tuple-element.38), channel_id=1, source_target_pairs={{0,1},{1,0},{2,3},{3,2},{4,5},{5,4},{6,7},{7,6},{8,9},{9,8},{10,11... | collective-permute-start | bytes 1572872 | tf_op jit(solution)/shard_map/ppermute | solution.py:22
  193.3 1.7 collective-permute-done.24.got_ref
  195.0 0.8 copy-done.9
  195.9 2.0 shard_map.116
  198.4 2.8 %collective-permute-start.26 = (bf16[128,512]{1,0:T(8,128)(2,1)}, bf16[128,512]{1,0:T(8,128)(2,1)S(1)}, u32[]{:S(2)}, u32[]{:S(2)}) collective-permute-start(bf16[128,512]{1,0:T(8,128)(2,1)} %get-tuple-element.41), channel_id=1, source_target_pairs={{0,128},{64,192},{128,0},{192,64},{1,129},{65,193},{129,1},{193,65... | collective-permute-start | bytes 393224 | tf_op jit(solution)/shard_map/ppermute | solution.py:22
  201.2 2.8 %collective-permute-done.25 = bf16[128,512]{1,0:T(8,128)(2,1)S(1)} collective-permute-done((bf16[128,512]{1,0:T(8,128)(2,1)}, bf16[128,512]{1,0:T(8,128)(2,1)S(1)}, u32[]{:S(2)}, u32[]{:S(2)}) %collective-permute-start.25) | collective-permute-done | bytes 131104 | tf_op jit(solution)/shard_map/ppermute | solution.py:22
  204.0 3.4 %collective-permute-done.26 = bf16[128,512]{1,0:T(8,128)(2,1)S(1)} collective-permute-done((bf16[128,512]{1,0:T(8,128)(2,1)}, bf16[128,512]{1,0:T(8,128)(2,1)S(1)}, u32[]{:S(2)}, u32[]{:S(2)}) %collective-permute-start.26) | collective-permute-done | bytes 131104 | tf_op jit(solution)/shard_map/ppermute | solution.py:22
  207.5 1.6 add_convert_fusion
  (89 shorter events, 12.1 us)
Async XLA Ops:
  6.5 69.7 %all-gather.4.cloned.1.call-start = ((), (), s32[]{:S(2)}) async-start(), calls=%async_computation.4 | async-start | bytes 2359296 | tf_op jit(solution)/shard_map/all_gather | solution.py:348
  8.8 15.3 %copy-start.20 = (bf16[1024,128]{1,0:T(8,128)(2,1)S(1)}, bf16[1024,128]{1,0:T(8,128)(2,1)}, u32[]{:S(2)}) copy-start(bf16[1024,128]{1,0:T(8,128)(2,1)} %param.21) | copy-start | bytes 786436
  8.8 16.0 %copy-start.15 = (bf16[128,512]{1,0:T(8,128)(2,1)S(1)}, bf16[128,512]{1,0:T(8,128)(2,1)}, u32[]{:S(2)}) copy-start(bf16[128,512]{1,0:T(8,128)(2,1)} %param.11) | copy-start | bytes 393220
  23.3 122.1 %all-gather.6.cloned.1.call-start = ((), (), s32[]{:S(2)}) async-start(), calls=%async_computation.5 | async-start | bytes 2359296 | tf_op jit(solution)/shard_map/all_gather | solution.py:349
  24.1 150.3 %all-gather.8.cloned.1.call-start = ((), (), s32[]{:S(2)}) async-start(), calls=%async_computation.6 | async-start | bytes 2359296 | tf_op jit(solution)/shard_map/all_gather | solution.py:384
  24.1 4.3 %collective-permute-start.23 = (bf16[1024,128]{1,0:T(8,128)(2,1)S(1)}, bf16[1024,128]{1,0:T(8,128)(2,1)S(1)}, u32[]{:S(2)}, u32[]{:S(2)}) collective-permute-start(bf16[1024,128]{1,0:T(8,128)(2,1)S(1)} %copy-done.20), channel_id=1, source_target_pairs={{0,0},{2,64},{4,128},{6,192},{64,2},{66,66},{68,130},{70,194},{128... | collective-permute-start | bytes 786440 | tf_op jit(solution)/shard_map/ppermute | solution.py:383
  24.8 4.4 %collective-permute-start = (bf16[16,512]{1,0:T(8,128)(2,1)S(1)}, bf16[16,512]{1,0:T(8,128)(2,1)S(1)}, u32[]{:S(2)}, u32[]{:S(2)}) collective-permute-start(bf16[16,512]{1,0:T(8,128)(2,1)S(1)} %slice.9), channel_id=1, source_target_pairs={{0,8},{8,16},{16,24},{24,32},{32,40},{40,48},{48,56},{56,64},{64,7... | collective-permute-start | bytes 49160 | tf_op jit(solution)/shard_map/ppermute | solution.py:304
  29.3 19.9 %collective-permute-start.1 = (bf16[144,512]{1,0:T(8,128)(2,1)S(1)}, bf16[144,512]{1,0:T(8,128)(2,1)S(1)}, u32[]{:S(2)}, u32[]{:S(2)}) collective-permute-start(bf16[144,512]{1,0:T(8,128)(2,1)S(1)} %get-tuple-element.45), channel_id=1, source_target_pairs={{0,64},{1,3},{2,66},{3,5},{4,68},{5,7},{6,70},{7,1},{64,128},{65,6... | collective-permute-start | bytes 442376 | tf_op jit(solution)/shard_map/ppermute | solution.py:315
  36.8 14.8 %collective-permute-start.2 = (bf16[144,512]{1,0:T(8,128)(2,1)S(1)}, bf16[144,512]{1,0:T(8,128)(2,1)S(1)}, u32[]{:S(2)}, u32[]{:S(2)}) collective-permute-start(bf16[144,512]{1,0:T(8,128)(2,1)S(1)} %get-tuple-element.45), channel_id=1, source_target_pairs={{0,128},{1,5},{2,130},{3,7},{4,132},{5,1},{6,134},{7,3},{64,192},{... | collective-permute-start | bytes 442376 | tf_op jit(solution)/shard_map/ppermute | solution.py:315
  47.4 4.4 %collective-permute-start.3 = (bf16[144,512]{1,0:T(8,128)(2,1)S(1)}, bf16[144,512]{1,0:T(8,128)(2,1)S(1)}, u32[]{:S(2)}, u32[]{:S(2)}) collective-permute-start(bf16[144,512]{1,0:T(8,128)(2,1)S(1)} %get-tuple-element.45), channel_id=1, source_target_pairs={{0,192},{1,7},{2,194},{3,1},{4,196},{5,3},{6,198},{7,5},{64,0},{65... | collective-permute-start | bytes 442376 | tf_op jit(solution)/shard_map/ppermute | solution.py:315
  51.8 24.4 %copy-start = (bf16[576,512]{1,0:T(8,128)(2,1)}, bf16[576,512]{1,0:T(8,128)(2,1)S(1)}, u32[]{:S(2)}) copy-start(bf16[576,512]{1,0:T(8,128)(2,1)S(1)} %constant_dynamic-update-slice_fusion.2.refs_0_) | copy-start | bytes 1769476
  51.8 9.1 %collective-permute-start.6 = (bf16[576,512]{1,0:T(8,128)(2,1)S(1)}, bf16[576,512]{1,0:T(8,128)(2,1)S(1)}, u32[]{:S(2)}, u32[]{:S(2)}) collective-permute-start(bf16[576,512]{1,0:T(8,128)(2,1)S(1)} %constant_dynamic-update-slice_fusion.2.refs_0_), channel_id=1, source_target_pairs={{0,6},{1,193},{2,0},{3,195},{4,2},{5,197},{6,4},{7,199},{64,70},{6... | collective-permute-start | bytes 1769480 | tf_op jit(solution)/shard_map/ppermute | solution.py:315
  52.4 17.5 %collective-permute-start.4 = (bf16[576,512]{1,0:T(8,128)(2,1)S(1)}, bf16[576,512]{1,0:T(8,128)(2,1)S(1)}, u32[]{:S(2)}, u32[]{:S(2)}) collective-permute-start(bf16[576,512]{1,0:T(8,128)(2,1)S(1)} %constant_dynamic-update-slice_fusion.2.refs_0_), channel_id=1, source_target_pairs={{0,2},{1,65},{2,4},{3,67},{4,6},{5,69},{6,0},{7,71},{64,66},{65,12... | collective-permute-start | bytes 1769480 | tf_op jit(solution)/shard_map/ppermute | solution.py:315
  53.4 20.3 %collective-permute-start.5 = (bf16[576,512]{1,0:T(8,128)(2,1)S(1)}, bf16[576,512]{1,0:T(8,128)(2,1)S(1)}, u32[]{:S(2)}, u32[]{:S(2)}) collective-permute-start(bf16[576,512]{1,0:T(8,128)(2,1)S(1)} %constant_dynamic-update-slice_fusion.2.refs_0_), channel_id=1, source_target_pairs={{0,4},{1,129},{2,6},{3,131},{4,0},{5,133},{6,2},{7,135},{64,68},{6... | collective-permute-start | bytes 1769480 | tf_op jit(solution)/shard_map/ppermute | solution.py:315
  53.7 20.7 %collective-permute-start.7 = (bf16[576,512]{1,0:T(8,128)(2,1)S(1)}, bf16[576,512]{1,0:T(8,128)(2,1)S(1)}, u32[]{:S(2)}, u32[]{:S(2)}) collective-permute-start(bf16[576,512]{1,0:T(8,128)(2,1)S(1)} %constant_dynamic-update-slice_fusion.2.refs_0_), channel_id=1, source_target_pairs={{0,1},{1,0},{2,3},{3,2},{4,5},{5,4},{6,7},{7,6},{8,9},{9,8},{10,11... | collective-permute-start | bytes 1769480 | tf_op jit(solution)/shard_map/ppermute | solution.py:22
  60.9 15.3 %copy-start.1 = (bf16[576,512]{1,0:T(8,128)(2,1)}, bf16[576,512]{1,0:T(8,128)(2,1)S(1)}, u32[]{:S(2)}) copy-start(bf16[576,512]{1,0:T(8,128)(2,1)S(1)} %collective-permute-done.6.refs_3_) | copy-start | bytes 1769476
  60.9 13.5 %collective-permute-start.10 = (bf16[576,512]{1,0:T(8,128)(2,1)S(1)}, bf16[576,512]{1,0:T(8,128)(2,1)S(1)}, u32[]{:S(2)}, u32[]{:S(2)}) collective-permute-start(bf16[576,512]{1,0:T(8,128)(2,1)S(1)} %collective-permute-done.6.refs_3_), channel_id=1, source_target_pairs={{0,1},{1,0},{2,3},{3,2},{4,5},{5,4},{6,7},{7,6},{8,9},{9,8},{10,11... | collective-permute-start | bytes 1769480 | tf_op jit(solution)/shard_map/ppermute | solution.py:22
  70.0 6.3 %copy-start.2 = (bf16[576,512]{1,0:T(8,128)(2,1)}, bf16[576,512]{1,0:T(8,128)(2,1)S(1)}, u32[]{:S(2)}) copy-start(bf16[576,512]{1,0:T(8,128)(2,1)S(1)} %collective-permute-done.4.refs_1_) | copy-start | bytes 1769476
  70.0 5.4 %collective-permute-start.8 = (bf16[576,512]{1,0:T(8,128)(2,1)S(1)}, bf16[576,512]{1,0:T(8,128)(2,1)}, u32[]{:S(2)}, u32[]{:S(2)}) collective-permute-start(bf16[576,512]{1,0:T(8,128)(2,1)S(1)} %collective-permute-done.4.refs_1_), channel_id=1, source_target_pairs={{0,1},{1,0},{2,3},{3,2},{4,5},{5,4},{6,7},{7,6},{8,9},{9,8},{10,11... | collective-permute-start | bytes 1769480 | tf_op jit(solution)/shard_map/ppermute | solution.py:22
  73.7 2.6 %copy-start.3 = (bf16[576,512]{1,0:T(8,128)(2,1)}, bf16[576,512]{1,0:T(8,128)(2,1)S(1)}, u32[]{:S(2)}) copy-start(bf16[576,512]{1,0:T(8,128)(2,1)S(1)} %collective-permute-done.5.refs_2_) | copy-start | bytes 1769476
  73.7 2.6 %collective-permute-start.9 = (bf16[576,512]{1,0:T(8,128)(2,1)S(1)}, bf16[576,512]{1,0:T(8,128)(2,1)}, u32[]{:S(2)}, u32[]{:S(2)}) collective-permute-start(bf16[576,512]{1,0:T(8,128)(2,1)S(1)} %collective-permute-done.5.refs_2_), channel_id=1, source_target_pairs={{0,1},{1,0},{2,3},{3,2},{4,5},{5,4},{6,7},{7,6},{8,9},{9,8},{10,11... | collective-permute-start | bytes 1769480 | tf_op jit(solution)/shard_map/ppermute | solution.py:22
  74.4 1.9 copy-start.4
  74.4 1.9 copy-start.5
  81.7 29.6 %copy-start.19 = (f32[1024,16]{0,1:T(8,128)S(1)}, f32[1024,16]{0,1:T(8,128)}, u32[]{:S(2)}) copy-start(f32[1024,16]{0,1:T(8,128)} %param.19) | copy-start | bytes 196612
  95.5 2.6 %collective-permute-start.11 = (f32[64,544]{1,0:T(8,128)}, f32[64,544]{1,0:T(8,128)S(1)}, u32[]{:S(2)}, u32[]{:S(2)}) collective-permute-start(f32[64,544]{1,0:T(8,128)} %get-tuple-element.26), channel_id=1, source_target_pairs={{0,1},{1,0},{2,3},{3,2},{4,5},{5,4},{6,7},{7,6},{8,9},{9,8},{10,11... | collective-permute-start | bytes 417800 | tf_op jit(solution)/shard_map/ppermute | solution.py:22
  99.0 10.4 %collective-permute-start.12 = (f32[64,544]{1,0:T(8,128)S(1)}, f32[64,544]{1,0:T(8,128)S(1)}, u32[]{:S(2)}, u32[]{:S(2)}) collective-permute-start(f32[64,544]{1,0:T(8,128)S(1)} %add.29), channel_id=1, source_target_pairs={{0,2},{2,4},{4,6},{6,0},{1,3},{3,5},{5,7},{7,1},{8,10},{10,12},{12... | collective-permute-start | bytes 417800 | tf_op jit(solution)/shard_map/ppermute | solution.py:22
  99.3 10.1 %collective-permute-start.13 = (f32[64,544]{1,0:T(8,128)S(1)}, f32[64,544]{1,0:T(8,128)S(1)}, u32[]{:S(2)}, u32[]{:S(2)}) collective-permute-start(f32[64,544]{1,0:T(8,128)S(1)} %add.29), channel_id=1, source_target_pairs={{0,4},{2,6},{4,0},{6,2},{1,5},{3,7},{5,1},{7,3},{8,12},{10,14},{12... | collective-permute-start | bytes 417800 | tf_op jit(solution)/shard_map/ppermute | solution.py:22
  101.0 8.8 %collective-permute-start.14 = (f32[64,544]{1,0:T(8,128)S(1)}, f32[64,544]{1,0:T(8,128)S(1)}, u32[]{:S(2)}, u32[]{:S(2)}) collective-permute-start(f32[64,544]{1,0:T(8,128)S(1)} %add.29), channel_id=1, source_target_pairs={{0,6},{2,0},{4,2},{6,4},{1,7},{3,1},{5,3},{7,5},{8,14},{10,8},{12,... | collective-permute-start | bytes 417800 | tf_op jit(solution)/shard_map/ppermute | solution.py:22
  109.8 2.6 %copy-start.6 = (f32[64,544]{1,0:T(8,128)}, f32[64,544]{1,0:T(8,128)S(1)}, u32[]{:S(2)}) copy-start(f32[64,544]{1,0:T(8,128)S(1)} %add_add_fusion.mine_ref) | copy-start | bytes 417796
  109.8 2.6 %collective-permute-start.15 = (f32[64,544]{1,0:T(8,128)S(1)}, f32[64,544]{1,0:T(8,128)S(1)}, u32[]{:S(2)}, u32[]{:S(2)}) collective-permute-start(f32[64,544]{1,0:T(8,128)S(1)} %add_add_fusion.mine_ref), channel_id=1, source_target_pairs={{0,1},{1,0},{2,3},{3,2},{4,5},{5,4},{6,7},{7,6},{8,9},{9,8},{10,11... | collective-permute-start | bytes 417800 | tf_op jit(solution)/shard_map/ppermute | solution.py:22
  142.1 17.1 %all-to-all-start.3 = ((bf16[4,18,8,128]{3,2,1,0:T(8,128)(2,1)}), bf16[4,18,8,128]{3,2,1,0:T(8,128)(2,1)S(1)}, u32[]{:S(2)}, u32[]{:S(2)}) async-start(bf16[4,18,8,128]{3,2,1,0:T(8,128)(2,1)} %get-tuple-element.30), calls=%async_computation.3 | async-start | bytes 294912 | tf_op jit(solution)/shard_map/all_to_all | solution.py:420
  150.7 4.3 %collective-permute-start.16 = (bf16[128,256]{1,0:T(8,128)(2,1)}, bf16[128,256]{1,0:T(8,128)(2,1)S(1)}, u32[]{:S(2)}, u32[]{:S(2)}) collective-permute-start(bf16[128,256]{1,0:T(8,128)(2,1)} %get-tuple-element.34), channel_id=1, source_target_pairs={{0,192},{64,0},{128,64},{192,128},{1,193},{65,1},{129,65},{193,129... | collective-permute-start | bytes 196616 | tf_op jit(solution)/shard_map/ppermute | solution.py:22
  153.3 4.9 %collective-permute-start.17 = (bf16[128,256]{1,0:T(8,128)(2,1)}, bf16[128,256]{1,0:T(8,128)(2,1)S(1)}, u32[]{:S(2)}, u32[]{:S(2)}) collective-permute-start(bf16[128,256]{1,0:T(8,128)(2,1)} %get-tuple-element.35), channel_id=1, source_target_pairs={{0,128},{64,192},{128,0},{192,64},{1,129},{65,193},{129,1},{193,65... | collective-permute-start | bytes 196616 | tf_op jit(solution)/shard_map/ppermute | solution.py:22
  153.9 5.4 %collective-permute-start.18 = (bf16[128,256]{1,0:T(8,128)(2,1)}, bf16[128,256]{1,0:T(8,128)(2,1)S(1)}, u32[]{:S(2)}, u32[]{:S(2)}) collective-permute-start(bf16[128,256]{1,0:T(8,128)(2,1)} %get-tuple-element.36), channel_id=1, source_target_pairs={{0,64},{64,128},{128,192},{192,0},{1,65},{65,129},{129,193},{193,1... | collective-permute-start | bytes 196616 | tf_op jit(solution)/shard_map/ppermute | solution.py:22
  154.9 4.3 %copy-start.16 = (bf16[128,256]{1,0:T(8,128)(2,1)}, bf16[128,256]{1,0:T(8,128)(2,1)S(1)}, u32[]{:S(2)}) copy-start(bf16[128,256]{1,0:T(8,128)(2,1)S(1)} %collective-permute-done.16.refs_1_) | copy-start | bytes 196612
  158.1 1.1 copy-start.17
  165.1 9.2 %collective-permute-start.19 = (bf16[128,1024]{1,0:T(8,128)(2,1)}, bf16[128,1024]{1,0:T(8,128)(2,1)S(1)}, u32[]{:S(2)}, u32[]{:S(2)}) collective-permute-start(bf16[128,1024]{1,0:T(8,128)(2,1)} %shard_map.114), channel_id=1, source_target_pairs={{0,0},{2,64},{4,128},{6,192},{64,2},{66,66},{68,130},{70,194},{128... | collective-permute-start | bytes 786440 | tf_op jit(solution)/shard_map/ppermute | solution.py:438
  166.7 18.0 %collective-permute-start.20 = (bf16[128,1024]{1,0:T(8,128)(2,1)}, bf16[128,1024]{1,0:T(8,128)(2,1)S(1)}, u32[]{:S(2)}, u32[]{:S(2)}) collective-permute-start(bf16[128,1024]{1,0:T(8,128)(2,1)} %shard_map.114), channel_id=1, source_target_pairs={{0,2},{2,66},{4,130},{6,194},{64,4},{66,68},{68,132},{70,196},{128... | collective-permute-start | bytes 786440 | tf_op jit(solution)/shard_map/ppermute | solution.py:438
  167.8 16.9 %collective-permute-start.21 = (bf16[128,1024]{1,0:T(8,128)(2,1)}, bf16[128,1024]{1,0:T(8,128)(2,1)S(1)}, u32[]{:S(2)}, u32[]{:S(2)}) collective-permute-start(bf16[128,1024]{1,0:T(8,128)(2,1)} %shard_map.114), channel_id=1, source_target_pairs={{0,4},{2,68},{4,132},{6,196},{64,6},{66,70},{68,134},{70,198},{128... | collective-permute-start | bytes 786440 | tf_op jit(solution)/shard_map/ppermute | solution.py:438
  170.7 14.0 %collective-permute-start.22 = (bf16[128,1024]{1,0:T(8,128)(2,1)}, bf16[128,1024]{1,0:T(8,128)(2,1)S(1)}, u32[]{:S(2)}, u32[]{:S(2)}) collective-permute-start(bf16[128,1024]{1,0:T(8,128)(2,1)} %shard_map.114), channel_id=1, source_target_pairs={{0,6},{2,70},{4,134},{6,198},{64,0},{66,64},{68,128},{70,192},{128... | collective-permute-start | bytes 786440 | tf_op jit(solution)/shard_map/ppermute | solution.py:438
  174.3 10.4 %copy-start.11 = (bf16[128,1024]{1,0:T(8,128)(2,1)}, bf16[128,1024]{1,0:T(8,128)(2,1)S(1)}, u32[]{:S(2)}) copy-start(bf16[128,1024]{1,0:T(8,128)(2,1)S(1)} %collective-permute-done.19.refs_0_) | copy-start | bytes 786436
  184.7 0.7 copy-start.12
  184.7 0.8 copy-start.13
  190.2 4.8 %collective-permute-start.24 = (bf16[4,128,512]{2,1,0:T(8,128)(2,1)}, bf16[4,128,512]{2,1,0:T(8,128)(2,1)S(1)}, u32[]{:S(2)}, u32[]{:S(2)}) collective-permute-start(bf16[4,128,512]{2,1,0:T(8,128)(2,1)} %get-tuple-element.38), channel_id=1, source_target_pairs={{0,1},{1,0},{2,3},{3,2},{4,5},{5,4},{6,7},{7,6},{8,9},{9,8},{10,11... | collective-permute-start | bytes 1572872 | tf_op jit(solution)/shard_map/ppermute | solution.py:22
  195.0 0.8 copy-start.9
  197.9 6.1 %collective-permute-start.25 = (bf16[128,512]{1,0:T(8,128)(2,1)}, bf16[128,512]{1,0:T(8,128)(2,1)S(1)}, u32[]{:S(2)}, u32[]{:S(2)}) collective-permute-start(bf16[128,512]{1,0:T(8,128)(2,1)} %get-tuple-element.40), channel_id=1, source_target_pairs={{0,64},{64,128},{128,192},{192,0},{1,65},{65,129},{129,193},{193,1... | collective-permute-start | bytes 393224 | tf_op jit(solution)/shard_map/ppermute | solution.py:22
  198.4 9.0 %collective-permute-start.26 = (bf16[128,512]{1,0:T(8,128)(2,1)}, bf16[128,512]{1,0:T(8,128)(2,1)S(1)}, u32[]{:S(2)}, u32[]{:S(2)}) collective-permute-start(bf16[128,512]{1,0:T(8,128)(2,1)} %get-tuple-element.41), channel_id=1, source_target_pairs={{0,128},{64,192},{128,0},{192,64},{1,129},{65,193},{129,1},{193,65... | collective-permute-start | bytes 393224 | tf_op jit(solution)/shard_map/ppermute | solution.py:22
  201.2 6.2 %collective-permute-start.27 = (bf16[128,512]{1,0:T(8,128)(2,1)}, bf16[128,512]{1,0:T(8,128)(2,1)S(1)}, u32[]{:S(2)}, u32[]{:S(2)}) collective-permute-start(bf16[128,512]{1,0:T(8,128)(2,1)} %get-tuple-element.42), channel_id=1, source_target_pairs={{0,192},{64,0},{128,64},{192,128},{1,193},{65,1},{129,65},{193,129... | collective-permute-start | bytes 393224 | tf_op jit(solution)/shard_map/ppermute | solution.py:22
  (5 other events, 3.4 us)
Sparse Core Ops, SparseCore 0:
  23.4 38.7 all-gather.3
  64.0 39.4 all-gather.5
  105.2 50.1 all-gather.7
where the time goes:
time: 217 us; the launch traced here: 216 us
  starting transfers between devices  69.7 us (32%)
  blocking collectives  47.1 us (22%)
  waiting for transfers between devices  42.8 us (20%)
  Pallas kernels  31 us (14%)
  between operations  13.4 us (6%)
  local copies, waits for them, and re-layouts  8.26 us (4%)
  other arithmetic  3.35 us (2%)
    ppermute x16, starting transfers between devices, shifted(): lax.ppermute(block, axis, [(i, (i + distance) % n) for i in range(n)])  32.9 us
    pallas_call x8, Pallas kernels, call(): pl.pallas_call(kernel, out_shape=out_shape, in_specs=[pl.BlockSpec(memory...  31 us
    ppermute x16, waiting for transfers between devices, shifted(): lax.ppermute(block, axis, [(i, (i + distance) % n) for i in range(n)])  24 us
    all_to_all x1, blocking collectives, on_device(): ends = lax.all_to_all(packed, 'z', 0, 0, tiled=True)  22.7 us
    ppermute x6, starting transfers between devices, spread_tokens(): got.append(lax.ppermute(block, ('y', 'x', 'c'), route))  20 us
    all_to_all x1, blocking collectives, on_device(): quarters = lax.all_to_all(quarters, 'y', 0, 0, tiled=True)  13.4 us
    all_to_all x1, blocking collectives, on_device(): conv_got = lax.all_to_all(conv_quad, 'y', 0, 0, tiled=True)  10.9 us
    ppermute x4, waiting for transfers between devices, on_device(): lax.ppermute(gated, ('y', 'x'), [(y * n + x, x * n + (y + r) % n) for y i...  10.3 us
  transfers between devices with their start and end apart: 32, of which 18 were waited for; matrix products, arithmetic and copies ran while one was open for 1% of the time, Pallas kernels for 12%

commit v1 on v0

--- a/solution.py
+++ b/solution.py
@@ -49,7 +49,7 @@
     return jax.ShapeDtypeStruct(shape, dtype)
 
 
-def project_pieces(n, place_ref, zero, one, w_ref):
+def project_pieces(n, place_ref, zero, one, w_ref, by_distance):
     width = zero[0].shape[1]
     rows = zero[0].shape[0] // n
     left = [
@@ -67,8 +67,9 @@
         weights = []
         for k in range(n):
             x = lax.rem(place_ref[X] + n - k, n)
+            at = lax.rem(place_ref[Y] + n - x, n) if by_distance else x
             for q in range(width // 128):
-                start = pl.multiple_of(((c * (width // 128) + q) * n + x) * 128, 128)
+                start = pl.multiple_of(((c * (width // 128) + q) * n + at) * 128, 128)
                 weights.append(w_ref[pl.ds(start, 128), :])
         weight = jnp.concatenate(weights, 0)
         product = jnp.dot(left[c], weight, preferred_element_type=jnp.float32)
@@ -80,7 +81,7 @@
     pieces, w_ref, out_ref, scale_ref = refs[: 2 * n], refs[2 * n], refs[-2], refs[-1]
 
     def finish(zero, one):
-        left, total = project_pieces(n, place_ref, zero, one, w_ref)
+        left, total = project_pieces(n, place_ref, zero, one, w_ref, True)
         rows = total.shape[0] // n
         for k in range(n):
             where = slice(k * rows, (k + 1) * rows)
@@ -103,7 +104,7 @@
     pieces, w_ref, scale_ref, outs = refs[: 2 * n], refs[2 * n], refs[2 * n + 1], refs[2 * n + 2 :]
 
     def finish(zero, one):
-        _, total = project_pieces(n, place_ref, zero, one, w_ref)
+        _, total = project_pieces(n, place_ref, zero, one, w_ref, False)
         rows = total.shape[0] // n
         for k in range(n):
             where = slice(k * rows + HALO, (k + 1) * rows)
@@ -341,12 +342,19 @@
 
     features = norm_gain.shape[0]
     count = in_proj.shape[0]
-    gain = lax.dynamic_slice_in_dim(norm_gain, lax.axis_index(SEQ) * count, count, 0)
+    first = lax.axis_index(SEQ) * count
+    gain = lax.dynamic_slice_in_dim(norm_gain, first, count, 0)
     gained = (in_proj.astype(jnp.float32) * gain[:, None, None]).astype(jnp.bfloat16)
-    quarters = gained.reshape(-1, 2, n, width).transpose(2, 1, 0, 3)
-    quarters = lax.all_to_all(quarters, "y", 0, 0, tiled=True)
-    conv_w = lax.all_gather(quarters[:, 0].reshape(-1, width), "z", axis=0, tiled=True)
-    gate_w = lax.all_gather(quarters[:, 1].reshape(-1, width), "z", axis=0, tiled=True)
+    conv_part = gained[:, 0]
+    mine = lax.axis_index("y")
+    parts = [
+        lax.dynamic_slice_in_dim(conv_part, (mine + k) % n * width, width, 1) for k in range(n)
+    ]
+    parts[1:] = [shifted(parts[k], "y", k) for k in range(1, n)]
+    conv_w = lax.all_gather(jnp.concatenate(parts, 0), "z", axis=0, tiled=True)
+    gate_part = gained[:, 1].reshape(count, n, width).transpose(1, 0, 2)
+    gate_part = lax.all_to_all(gate_part, "y", 0, 0, tiled=True)
+    gate_w = lax.all_gather(gate_part.reshape(-1, width), "z", axis=0, tiled=True)
 
     own = spread_tokens(tokens)
     pieces = own + [shifted(own[0], "c", 1)]
@@ -375,8 +383,8 @@
         scratch=[pltpu.VMEM((local_tokens, features_out), jnp.float32)],
     )
     pair = kept + shifted(given, "c", 1)
-    behind = from_behind(pair, "x")
-    mine = sum(behind[1:], pair)
+    behind = from_behind(pair.astype(jnp.bfloat16), "x")
+    mine = sum((piece.astype(jnp.float32) for piece in behind[1:]), pair)
     theirs = shifted(mine, "c", 1)
 
     swap = [(y * n + x, x * n + y) for y in range(n) for x in range(n)]

time: 217 us -> 221 us (1.018)
  starting transfers between devices: 69.7 us -> 81.7 us
  blocking collectives: 47.1 us -> 42.6 us
  waiting for transfers between devices: 42.8 us -> 38.7 us
    ppermute x16 -> x19, starting transfers between devices: 32.9 us -> 43.2 us  [shifted(): lax.ppermute(block, axis, [(i, (i + distance) % n) for i in range(n)])]
    all_to_all x1, blocking collectives: 13.4 us -> 8.58 us  [on_device(): gate_part = lax.all_to_all(gate_part, 'y', 0, 0, tiled=True)]
    ppermute x6, starting transfers between devices: 20 us -> 22.4 us  [spread_tokens(): got.append(lax.ppermute(block, ('y', 'x', 'c'), route))]
    ppermute x16 -> x19, waiting for transfers between devices: 24 us -> 22.3 us  [shifted(): lax.ppermute(block, axis, [(i, (i + distance) % n) for i in range(n)])]
    unnamed x47 -> x46, local copies, waits for them, and re-layouts: 6.4 us -> 4.7 us
  transfers between devices with their start and end apart: 32 -> 35, of which waited for: 18 -> 19; matrix products, arithmetic and copies ran while one was open for 1% -> 2% of each run, Pallas kernels for 12% -> 11%
where the time goes in v1:
time: 221 us; the launch traced here: 219 us
  starting transfers between devices  81.7 us (37%)
  blocking collectives  42.6 us (19%)
  waiting for transfers between devices  38.7 us (18%)
  Pallas kernels  31.2 us (14%)
  between operations  13.4 us (6%)
  local copies, waits for them, and re-layouts  6.61 us (3%)
  other arithmetic  5.25 us (2%)
    ppermute x19, starting transfers between devices, shifted(): lax.ppermute(block, axis, [(i, (i + distance) % n) for i in range(n)])  43.2 us
    pallas_call x8, Pallas kernels, call(): pl.pallas_call(kernel, out_shape=out_shape, in_specs=[pl.BlockSpec(memory...  31.2 us
    all_to_all x1, blocking collectives, on_device(): ends = lax.all_to_all(packed, 'z', 0, 0, tiled=True)  23.1 us
    ppermute x6, starting transfers between devices, spread_tokens(): got.append(lax.ppermute(block, ('y', 'x', 'c'), route))  22.4 us
    ppermute x19, waiting for transfers between devices, shifted(): lax.ppermute(block, axis, [(i, (i + distance) % n) for i in range(n)])  22.3 us
    all_to_all x1, blocking collectives, on_device(): conv_got = lax.all_to_all(conv_quad, 'y', 0, 0, tiled=True)  10.9 us
    ppermute x4, waiting for transfers between devices, on_device(): lax.ppermute(gated, ('y', 'x'), [(y * n + x, x * n + (y + r) % n) for y i...  9.47 us
    all_to_all x1, blocking collectives, on_device(): gate_part = lax.all_to_all(gate_part, 'y', 0, 0, tiled=True)  8.58 us
  transfers between devices with their start and end apart: 35, of which 19 were waited for; matrix products, arithmetic and copies ran while one was open for 2% of the time, Pallas kernels for 11%

profile of v1, /device:TPU:1, one launch (start us, length us, event | category | flops | bytes accessed | tf_op | source)
XLA Modules:
  0.0 219.5 jit_solution(17147215265411104554)
XLA Ops:
  7.3 1.2 multiply_convert_fusion
  8.6 2.2 collective-permute-start.11
  10.8 2.6 %collective-permute-start.12 = (bf16[128,256]{1,0:T(8,128)(2,1)S(1)}, bf16[128,256]{1,0:T(8,128)(2,1)S(1)}, u32[]{:S(2)}, u32[]{:S(2)}) collective-permute-start(bf16[128,256]{1,0:T(8,128)(2,1)S(1)} %get-tuple-element.49), channel_id=1, source_target_pairs={{0,128},{64,192},{128,0},{192,64},{1,129},{65,193},{129,1},{193,65... | collective-permute-start | bytes 196616 | tf_op jit(solution)/shard_map/ppermute | solution.py:22
  13.5 1.1 collective-permute-start.13
  14.5 1.5 collective-permute-done.12
  17.8 8.6 %all_to_all.20 = bf16[4,128,256]{1,2,0:T(8,128)(2,1)S(1)} all-to-all(bf16[4,128,256]{1,2,0:T(8,128)(2,1)S(1)} %bitcast.29), channel_id=1, replica_groups=mesh['y'=4,'z'=8,'x'=4,'c'=2] {'y'}, dimensions={0} | all-to-all | bytes 524288 | tf_op jit(solution)/shard_map/all_to_all | solution.py:356
  27.4 3.6 %collective-permute-start = (bf16[16,512]{1,0:T(8,128)(2,1)S(1)}, bf16[16,512]{1,0:T(8,128)(2,1)S(1)}, u32[]{:S(2)}, u32[]{:S(2)}) collective-permute-start(bf16[16,512]{1,0:T(8,128)(2,1)S(1)} %slice.9), channel_id=1, source_target_pairs={{0,8},{8,16},{16,24},{24,32},{32,40},{40,48},{48,56},{56,64},{64,7... | collective-permute-start | bytes 49160 | tf_op jit(solution)/shard_map/ppermute | solution.py:305
  31.9 2.6 %collective-permute-start.1 = (bf16[144,512]{1,0:T(8,128)(2,1)S(1)}, bf16[144,512]{1,0:T(8,128)(2,1)S(1)}, u32[]{:S(2)}, u32[]{:S(2)}) collective-permute-start(bf16[144,512]{1,0:T(8,128)(2,1)S(1)} %get-tuple-element.51), channel_id=1, source_target_pairs={{0,64},{1,3},{2,66},{3,5},{4,68},{5,7},{6,70},{7,1},{64,128},{65,6... | collective-permute-start | bytes 442376 | tf_op jit(solution)/shard_map/ppermute | solution.py:316
  35.3 12.0 %collective-permute-start.2 = (bf16[144,512]{1,0:T(8,128)(2,1)S(1)}, bf16[144,512]{1,0:T(8,128)(2,1)S(1)}, u32[]{:S(2)}, u32[]{:S(2)}) collective-permute-start(bf16[144,512]{1,0:T(8,128)(2,1)S(1)} %get-tuple-element.51), channel_id=1, source_target_pairs={{0,128},{1,5},{2,130},{3,7},{4,132},{5,1},{6,134},{7,3},{64,192},{... | collective-permute-start | bytes 442376 | tf_op jit(solution)/shard_map/ppermute | solution.py:316
  47.3 6.3 %collective-permute-start.3 = (bf16[144,512]{1,0:T(8,128)(2,1)S(1)}, bf16[144,512]{1,0:T(8,128)(2,1)S(1)}, u32[]{:S(2)}, u32[]{:S(2)}) collective-permute-start(bf16[144,512]{1,0:T(8,128)(2,1)S(1)} %get-tuple-element.51), channel_id=1, source_target_pairs={{0,192},{1,7},{2,194},{3,1},{4,196},{5,3},{6,198},{7,5},{64,0},{65... | collective-permute-start | bytes 442376 | tf_op jit(solution)/shard_map/ppermute | solution.py:316
  53.6 5.0 %collective-permute-done.3 = bf16[144,512]{1,0:T(8,128)(2,1)S(1)} collective-permute-done((bf16[144,512]{1,0:T(8,128)(2,1)S(1)}, bf16[144,512]{1,0:T(8,128)(2,1)S(1)}, u32[]{:S(2)}, u32[]{:S(2)}) %collective-permute-start.3) | collective-permute-done | bytes 147488 | tf_op jit(solution)/shard_map/ppermute | solution.py:316
  58.7 1.5 collective-permute-start.4
  60.1 5.8 %collective-permute-start.7 = (bf16[576,512]{1,0:T(8,128)(2,1)S(1)}, bf16[576,512]{1,0:T(8,128)(2,1)S(1)}, u32[]{:S(2)}, u32[]{:S(2)}) collective-permute-start(bf16[576,512]{1,0:T(8,128)(2,1)S(1)} %constant_dynamic-update-slice_fusion.2.refs_0_), channel_id=1, source_target_pairs={{0,1},{1,0},{2,3},{3,2},{4,5},{5,4},{6,7},{7,6},{8,9},{9,8},{10,11... | collective-permute-start | bytes 1769480 | tf_op jit(solution)/shard_map/ppermute | solution.py:22
  66.0 1.7 collective-permute-done.6.refs_3_
  67.7 10.4 %collective-permute-start.10 = (bf16[576,512]{1,0:T(8,128)(2,1)S(1)}, bf16[576,512]{1,0:T(8,128)(2,1)S(1)}, u32[]{:S(2)}, u32[]{:S(2)}) collective-permute-start(bf16[576,512]{1,0:T(8,128)(2,1)S(1)} %collective-permute-done.6.refs_3_), channel_id=1, source_target_pairs={{0,1},{1,0},{2,3},{3,2},{4,5},{5,4},{6,7},{7,6},{8,9},{9,8},{10,11... | collective-permute-start | bytes 1769480 | tf_op jit(solution)/shard_map/ppermute | solution.py:22
  78.2 3.7 %collective-permute-start.8 = (bf16[576,512]{1,0:T(8,128)(2,1)S(1)}, bf16[576,512]{1,0:T(8,128)(2,1)}, u32[]{:S(2)}, u32[]{:S(2)}) collective-permute-start(bf16[576,512]{1,0:T(8,128)(2,1)S(1)} %collective-permute-done.4.refs_1_), channel_id=1, source_target_pairs={{0,1},{1,0},{2,3},{3,2},{4,5},{5,4},{6,7},{7,6},{8,9},{9,8},{10,11... | collective-permute-start | bytes 1769480 | tf_op jit(solution)/shard_map/ppermute | solution.py:22
  84.5 5.6 %shard_map.109 = (bf16[4,144,256]{2,1,0:T(8,128)(2,1)}, f32[576,128]{1,0:T(8,128)}) custom-call(s32[4]{0:T(128)} %pad_add_fusion.place_ref, bf16[576,512]{1,0:T(8,128)(2,1)} %copy-done, bf16[576,512]{1,0:T(8,128)(2,1)} %copy-done.2, bf16[576,512]{1,0:T(8,128)(2,1)} %copy-done.3, bf16[576,512]{1,0:T(8,128)(2,1)} %copy-done.1, bf16[576,512]{1,0:T(8,128)(2,1)} %copy-done.4, ...), custom_call_target="tpu_custom_call" | custom-call | tf_op jit(solution)/shard_map/pallas_call | solution.py:39
  90.1 10.9 %all_to_all.21.got_ref = bf16[4,144,256]{2,1,0:T(8,128)(2,1)} all-to-all(bf16[4,144,256]{2,1,0:T(8,128)(2,1)} %get-tuple-element.24), channel_id=1, replica_groups=mesh['y'=4,'z'=8,'x'=4,'c'=2] {'y'}, dimensions={0} | all-to-all | bytes 589824 | tf_op jit(solution)/shard_map/all_to_all | solution.py:370
  101.0 2.8 %shard_map.110 = (f32[1024,128]{1,0:T(8,128)}, f32[64,544]{1,0:T(8,128)}, f32[64,544]{1,0:T(8,128)}) custom-call(s32[4]{0:T(128)} %pad_add_fusion.place_ref, bf16[4,144,256]{2,1,0:T(8,128)(2,1)} %all_to_all.21.got_ref, f32[4,1024]{1,0:T(4,128)} %w_ref.1, f32[1,1024]{1,0:T(1,128)} %bitcast.30, bf16[544,1024]{1,0:T(8,128)(2,1)} %bitcast.24), custom_call_target="tpu_custom_call" | custom-call | tf_op jit(solution)/shard_map/pallas_call | solution.py:39
  103.8 1.3 collective-permute-start.14
  105.2 1.2 collective-permute-done.14
  106.4 1.0 fusion
  107.4 1.7 collective-permute-start.16
  109.2 0.9 collective-permute-start.17
  110.1 4.1 %collective-permute-done.15 = bf16[64,544]{1,0:T(8,128)(2,1)S(1)} collective-permute-done((bf16[64,544]{1,0:T(8,128)(2,1)S(1)}, bf16[64,544]{1,0:T(8,128)(2,1)S(1)}, u32[]{:S(2)}, u32[]{:S(2)}) %collective-permute-start.15) | collective-permute-done | bytes 69664 | tf_op jit(solution)/shard_map/ppermute | solution.py:22
  114.4 1.6 collective-permute-start.18
  117.7 4.5 %shard_map.111 = (f32[1024,128]{1,0:T(8,128)}, bf16[8,18,8,128]{3,2,1,0:T(8,128)(2,1)}) custom-call(s32[4]{0:T(128)} %pad_add_fusion.place_ref, f32[64,544]{1,0:T(8,128)} %copy-done.6, f32[64,544]{1,0:T(8,128)} %copy-done.7, bf16[512,1024]{1,0:T(8,128)(2,1)} %dt_ref.1, f32[1,1024]{1,0:T(1,128)} %bitcast.31, f32[1024,128]{1,0:T(8,128)} %get-tuple-element.27.act_ref, ...), custom_call_target="tpu_custom_call" | custom-call | tf_op jit(solution)/shard_map/pallas_call | solution.py:39
  122.2 23.1 %all_to_all.22.got_ref = bf16[8,18,8,128]{3,2,1,0:T(8,128)(2,1)} all-to-all(bf16[8,18,8,128]{3,2,1,0:T(8,128)(2,1)} %get-tuple-element.29), channel_id=1, replica_groups=mesh['y'=4,'z'=8,'x'=4,'c'=2] {'z'}, dimensions={0} | all-to-all | bytes 589824 | tf_op jit(solution)/shard_map/all_to_all | solution.py:420
  145.3 1.8 shard_map.112
  147.1 3.3 %all-to-all-start.2 = ((bf16[4,18,8,128]{3,2,1,0:T(8,128)(2,1)}), bf16[4,18,8,128]{3,2,1,0:T(8,128)(2,1)S(1)}, u32[]{:S(2)}, u32[]{:S(2)}) async-start(bf16[4,18,8,128]{3,2,1,0:T(8,128)(2,1)} %get-tuple-element.30), calls=%async_computation.2 | async-start | bytes 294912 | tf_op jit(solution)/shard_map/all_to_all | solution.py:428
  150.5 5.2 %shard_map.113 = (bf16[128,256]{1,0:T(8,128)(2,1)}, bf16[128,256]{1,0:T(8,128)(2,1)}, bf16[128,256]{1,0:T(8,128)(2,1)}, bf16[128,256]{1,0:T(8,128)(2,1)}) custom-call(s32[4]{0:T(128)} %pad_add_fusion.place_ref, bf16[576,512]{1,0:T(8,128)(2,1)} %copy-done, bf16[576,512]{1,0:T(8,128)(2,1)} %copy-done.2, bf16[576,512]{1,0:T(8,128)(2,1)} %copy-done.3, ...), custom_call_target="tpu_custom_call" | custom-call | tf_op jit(solution)/shard_map/pallas_call | solution.py:39
  155.6 2.6 %collective-permute-start.19 = (bf16[128,256]{1,0:T(8,128)(2,1)}, bf16[128,256]{1,0:T(8,128)(2,1)S(1)}, u32[]{:S(2)}, u32[]{:S(2)}) collective-permute-start(bf16[128,256]{1,0:T(8,128)(2,1)} %get-tuple-element.34), channel_id=1, source_target_pairs={{0,192},{64,0},{128,64},{192,128},{1,193},{65,1},{129,65},{193,129... | collective-permute-start | bytes 196616 | tf_op jit(solution)/shard_map/ppermute | solution.py:22
  159.9 3.2 %collective-permute-done.20.refs_2_ = bf16[128,256]{1,0:T(8,128)(2,1)S(1)} collective-permute-done((bf16[128,256]{1,0:T(8,128)(2,1)}, bf16[128,256]{1,0:T(8,128)(2,1)S(1)}, u32[]{:S(2)}, u32[]{:S(2)}) %collective-permute-start.20) | collective-permute-done | bytes 65568 | tf_op jit(solution)/shard_map/ppermute | solution.py:22
  164.5 5.2 %shard_map.114 = bf16[128,1024]{1,0:T(8,128)(2,1)} custom-call(s32[4]{0:T(128)} %pad_add_fusion.place_ref, f32[64,544]{1,0:T(8,128)} %copy-done.6, f32[64,544]{1,0:T(8,128)} %copy-done.7, f32[1024,128]{1,0:T(8,128)} %get-tuple-element.28.step_ref, f32[1024,128]{1,0:T(8,128)} %get-tuple-element.27.act_ref, f32[16,8,128]{2,1,0:T(8,128)} %bitcast.27, ...), custom_call_target="tpu_custom_call" | custom-call | tf_op jit(solution)/shard_map/pallas_call | solution.py:39
  169.7 1.6 collective-permute-start.22
  171.3 1.0 collective-permute-start.23
  172.3 3.2 %collective-permute-start.24 = (bf16[128,1024]{1,0:T(8,128)(2,1)}, bf16[128,1024]{1,0:T(8,128)(2,1)S(1)}, u32[]{:S(2)}, u32[]{:S(2)}) collective-permute-start(bf16[128,1024]{1,0:T(8,128)(2,1)} %shard_map.114), channel_id=1, source_target_pairs={{0,4},{2,68},{4,132},{6,196},{64,6},{66,70},{68,134},{70,198},{128... | collective-permute-start | bytes 786440 | tf_op jit(solution)/shard_map/ppermute | solution.py:446
  175.4 2.6 %collective-permute-start.25 = (bf16[128,1024]{1,0:T(8,128)(2,1)}, bf16[128,1024]{1,0:T(8,128)(2,1)S(1)}, u32[]{:S(2)}, u32[]{:S(2)}) collective-permute-start(bf16[128,1024]{1,0:T(8,128)(2,1)} %shard_map.114), channel_id=1, source_target_pairs={{0,6},{2,70},{4,134},{6,198},{64,0},{66,64},{68,128},{70,192},{128... | collective-permute-start | bytes 786440 | tf_op jit(solution)/shard_map/ppermute | solution.py:446
  178.1 9.1 %collective-permute-done.23.refs_1_ = bf16[128,1024]{1,0:T(8,128)(2,1)S(1)} collective-permute-done((bf16[128,1024]{1,0:T(8,128)(2,1)}, bf16[128,1024]{1,0:T(8,128)(2,1)S(1)}, u32[]{:S(2)}, u32[]{:S(2)}) %collective-permute-start.23) | collective-permute-done | bytes 262176 | tf_op jit(solution)/shard_map/ppermute | solution.py:446
  188.7 4.0 %shard_map.115 = (bf16[4,128,512]{2,1,0:T(8,128)(2,1)}, bf16[4,128,512]{2,1,0:T(8,128)(2,1)}) custom-call(s32[4]{0:T(128)} %pad_add_fusion.place_ref, bf16[128,1024]{1,0:T(8,128)(2,1)} %copy-done.11, bf16[128,1024]{1,0:T(8,128)(2,1)} %copy-done.12, bf16[128,1024]{1,0:T(8,128)(2,1)} %copy-done.13, bf16[128,1024]{1,0:T(8,128)(2,1)} %copy-done.14, ...), custom_call_target="tpu_custom_call" | custom-call | tf_op jit(solution)/shard_map/pallas_call | solution.py:39
  192.7 2.6 %collective-permute-start.27 = (bf16[4,128,512]{2,1,0:T(8,128)(2,1)}, bf16[4,128,512]{2,1,0:T(8,128)(2,1)S(1)}, u32[]{:S(2)}, u32[]{:S(2)}) collective-permute-start(bf16[4,128,512]{2,1,0:T(8,128)(2,1)} %get-tuple-element.38), channel_id=1, source_target_pairs={{0,1},{1,0},{2,3},{3,2},{4,5},{5,4},{6,7},{7,6},{8,9},{9,8},{10,11... | collective-permute-start | bytes 1572872 | tf_op jit(solution)/shard_map/ppermute | solution.py:22
  195.3 1.7 collective-permute-done.27.got_ref
  197.8 2.0 shard_map.116
  199.9 2.4 %collective-permute-start.28 = (bf16[128,512]{1,0:T(8,128)(2,1)}, bf16[128,512]{1,0:T(8,128)(2,1)S(1)}, u32[]{:S(2)}, u32[]{:S(2)}) collective-permute-start(bf16[128,512]{1,0:T(8,128)(2,1)} %get-tuple-element.40), channel_id=1, source_target_pairs={{0,64},{64,128},{128,192},{192,0},{1,65},{65,129},{129,193},{193,1... | collective-permute-start | bytes 393224 | tf_op jit(solution)/shard_map/ppermute | solution.py:22
  202.3 2.8 %collective-permute-start.29 = (bf16[128,512]{1,0:T(8,128)(2,1)}, bf16[128,512]{1,0:T(8,128)(2,1)S(1)}, u32[]{:S(2)}, u32[]{:S(2)}) collective-permute-start(bf16[128,512]{1,0:T(8,128)(2,1)} %get-tuple-element.41), channel_id=1, source_target_pairs={{0,128},{64,192},{128,0},{192,64},{1,129},{65,193},{129,1},{193,65... | collective-permute-start | bytes 393224 | tf_op jit(solution)/shard_map/ppermute | solution.py:22
  205.1 2.5 %collective-permute-done.28 = bf16[128,512]{1,0:T(8,128)(2,1)S(1)} collective-permute-done((bf16[128,512]{1,0:T(8,128)(2,1)}, bf16[128,512]{1,0:T(8,128)(2,1)S(1)}, u32[]{:S(2)}, u32[]{:S(2)}) %collective-permute-start.28) | collective-permute-done | bytes 131104 | tf_op jit(solution)/shard_map/ppermute | solution.py:22
  207.6 3.7 %collective-permute-done.29 = bf16[128,512]{1,0:T(8,128)(2,1)S(1)} collective-permute-done((bf16[128,512]{1,0:T(8,128)(2,1)}, bf16[128,512]{1,0:T(8,128)(2,1)S(1)}, u32[]{:S(2)}, u32[]{:S(2)}) %collective-permute-start.29) | collective-permute-done | bytes 131104 | tf_op jit(solution)/shard_map/ppermute | solution.py:22
  211.3 1.6 add_convert_fusion
  (97 shorter events, 15.1 us)
Async XLA Ops:
  6.5 77.9 %all-gather.4.cloned.1.call-start = ((), (), s32[]{:S(2)}) async-start(), calls=%async_computation.4 | async-start | bytes 2359296 | tf_op jit(solution)/shard_map/all_gather | solution.py:354
  8.5 18.9 %copy-start.15 = (bf16[128,512]{1,0:T(8,128)(2,1)S(1)}, bf16[128,512]{1,0:T(8,128)(2,1)}, u32[]{:S(2)}) copy-start(bf16[128,512]{1,0:T(8,128)(2,1)} %param.11) | copy-start | bytes 393220
  8.5 22.5 %copy-start.20 = (bf16[1024,128]{1,0:T(8,128)(2,1)S(1)}, bf16[1024,128]{1,0:T(8,128)(2,1)}, u32[]{:S(2)}) copy-start(bf16[1024,128]{1,0:T(8,128)(2,1)} %param.21) | copy-start | bytes 786436
  8.6 5.9 %collective-permute-start.11 = (bf16[128,256]{1,0:T(8,128)(2,1)S(1)}, bf16[128,256]{1,0:T(8,128)(2,1)S(1)}, u32[]{:S(2)}, u32[]{:S(2)}) collective-permute-start(bf16[128,256]{1,0:T(8,128)(2,1)S(1)} %get-tuple-element.50), channel_id=1, source_target_pairs={{0,64},{64,128},{128,192},{192,0},{1,65},{65,129},{129,193},{193,1... | collective-permute-start | bytes 196616 | tf_op jit(solution)/shard_map/ppermute | solution.py:22
  10.8 5.2 %collective-permute-start.12 = (bf16[128,256]{1,0:T(8,128)(2,1)S(1)}, bf16[128,256]{1,0:T(8,128)(2,1)S(1)}, u32[]{:S(2)}, u32[]{:S(2)}) collective-permute-start(bf16[128,256]{1,0:T(8,128)(2,1)S(1)} %get-tuple-element.49), channel_id=1, source_target_pairs={{0,128},{64,192},{128,0},{192,64},{1,129},{65,193},{129,1},{193,65... | collective-permute-start | bytes 196616 | tf_op jit(solution)/shard_map/ppermute | solution.py:22
  13.5 3.4 %collective-permute-start.13 = (bf16[128,256]{1,0:T(8,128)(2,1)S(1)}, bf16[128,256]{1,0:T(8,128)(2,1)S(1)}, u32[]{:S(2)}, u32[]{:S(2)}) collective-permute-start(bf16[128,256]{1,0:T(8,128)(2,1)S(1)} %get-tuple-element.48), channel_id=1, source_target_pairs={{0,192},{64,0},{128,64},{192,128},{1,193},{65,1},{129,65},{193,129... | collective-permute-start | bytes 196616 | tf_op jit(solution)/shard_map/ppermute | solution.py:22
  17.6 132.8 %all-gather.6.cloned.1.call-start = ((), (), s32[]{:S(2)}) async-start(), calls=%async_computation.5 | async-start | bytes 2359296 | tf_op jit(solution)/shard_map/all_gather | solution.py:357
  27.3 150.8 %all-gather.8.cloned.1.call-start = ((), (), s32[]{:S(2)}) async-start(), calls=%async_computation.6 | async-start | bytes 2359296 | tf_op jit(solution)/shard_map/all_gather | solution.py:392
  27.4 4.5 %collective-permute-start = (bf16[16,512]{1,0:T(8,128)(2,1)S(1)}, bf16[16,512]{1,0:T(8,128)(2,1)S(1)}, u32[]{:S(2)}, u32[]{:S(2)}) collective-permute-start(bf16[16,512]{1,0:T(8,128)(2,1)S(1)} %slice.9), channel_id=1, source_target_pairs={{0,8},{8,16},{16,24},{24,32},{32,40},{40,48},{48,56},{56,64},{64,7... | collective-permute-start | bytes 49160 | tf_op jit(solution)/shard_map/ppermute | solution.py:305
  31.0 3.5 %collective-permute-start.26 = (bf16[1024,128]{1,0:T(8,128)(2,1)S(1)}, bf16[1024,128]{1,0:T(8,128)(2,1)S(1)}, u32[]{:S(2)}, u32[]{:S(2)}) collective-permute-start(bf16[1024,128]{1,0:T(8,128)(2,1)S(1)} %copy-done.20), channel_id=1, source_target_pairs={{0,0},{2,64},{4,128},{6,192},{64,2},{66,66},{68,130},{70,194},{128... | collective-permute-start | bytes 786440 | tf_op jit(solution)/shard_map/ppermute | solution.py:391
  31.9 21.6 %collective-permute-start.1 = (bf16[144,512]{1,0:T(8,128)(2,1)S(1)}, bf16[144,512]{1,0:T(8,128)(2,1)S(1)}, u32[]{:S(2)}, u32[]{:S(2)}) collective-permute-start(bf16[144,512]{1,0:T(8,128)(2,1)S(1)} %get-tuple-element.51), channel_id=1, source_target_pairs={{0,64},{1,3},{2,66},{3,5},{4,68},{5,7},{6,70},{7,1},{64,128},{65,6... | collective-permute-start | bytes 442376 | tf_op jit(solution)/shard_map/ppermute | solution.py:316
  35.3 18.2 %collective-permute-start.2 = (bf16[144,512]{1,0:T(8,128)(2,1)S(1)}, bf16[144,512]{1,0:T(8,128)(2,1)S(1)}, u32[]{:S(2)}, u32[]{:S(2)}) collective-permute-start(bf16[144,512]{1,0:T(8,128)(2,1)S(1)} %get-tuple-element.51), channel_id=1, source_target_pairs={{0,128},{1,5},{2,130},{3,7},{4,132},{5,1},{6,134},{7,3},{64,192},{... | collective-permute-start | bytes 442376 | tf_op jit(solution)/shard_map/ppermute | solution.py:316
  47.3 11.3 %collective-permute-start.3 = (bf16[144,512]{1,0:T(8,128)(2,1)S(1)}, bf16[144,512]{1,0:T(8,128)(2,1)S(1)}, u32[]{:S(2)}, u32[]{:S(2)}) collective-permute-start(bf16[144,512]{1,0:T(8,128)(2,1)S(1)} %get-tuple-element.51), channel_id=1, source_target_pairs={{0,192},{1,7},{2,194},{3,1},{4,196},{5,3},{6,198},{7,5},{64,0},{65... | collective-permute-start | bytes 442376 | tf_op jit(solution)/shard_map/ppermute | solution.py:316
  58.6 25.9 %copy-start = (bf16[576,512]{1,0:T(8,128)(2,1)}, bf16[576,512]{1,0:T(8,128)(2,1)S(1)}, u32[]{:S(2)}) copy-start(bf16[576,512]{1,0:T(8,128)(2,1)S(1)} %constant_dynamic-update-slice_fusion.2.refs_0_) | copy-start | bytes 1769476
  58.6 9.1 %collective-permute-start.6 = (bf16[576,512]{1,0:T(8,128)(2,1)S(1)}, bf16[576,512]{1,0:T(8,128)(2,1)S(1)}, u32[]{:S(2)}, u32[]{:S(2)}) collective-permute-start(bf16[576,512]{1,0:T(8,128)(2,1)S(1)} %constant_dynamic-update-slice_fusion.2.refs_0_), channel_id=1, source_target_pairs={{0,6},{1,193},{2,0},{3,195},{4,2},{5,197},{6,4},{7,199},{64,70},{6... | collective-permute-start | bytes 1769480 | tf_op jit(solution)/shard_map/ppermute | solution.py:316
  58.7 19.5 %collective-permute-start.4 = (bf16[576,512]{1,0:T(8,128)(2,1)S(1)}, bf16[576,512]{1,0:T(8,128)(2,1)S(1)}, u32[]{:S(2)}, u32[]{:S(2)}) collective-permute-start(bf16[576,512]{1,0:T(8,128)(2,1)S(1)} %constant_dynamic-update-slice_fusion.2.refs_0_), channel_id=1, source_target_pairs={{0,2},{1,65},{2,4},{3,67},{4,6},{5,69},{6,0},{7,71},{64,66},{65,12... | collective-permute-start | bytes 1769480 | tf_op jit(solution)/shard_map/ppermute | solution.py:316
  60.1 21.7 %collective-permute-start.5 = (bf16[576,512]{1,0:T(8,128)(2,1)S(1)}, bf16[576,512]{1,0:T(8,128)(2,1)S(1)}, u32[]{:S(2)}, u32[]{:S(2)}) collective-permute-start(bf16[576,512]{1,0:T(8,128)(2,1)S(1)} %constant_dynamic-update-slice_fusion.2.refs_0_), channel_id=1, source_target_pairs={{0,4},{1,129},{2,6},{3,131},{4,0},{5,133},{6,2},{7,135},{64,68},{6... | collective-permute-start | bytes 1769480 | tf_op jit(solution)/shard_map/ppermute | solution.py:316
  60.1 22.5 %collective-permute-start.7 = (bf16[576,512]{1,0:T(8,128)(2,1)S(1)}, bf16[576,512]{1,0:T(8,128)(2,1)S(1)}, u32[]{:S(2)}, u32[]{:S(2)}) collective-permute-start(bf16[576,512]{1,0:T(8,128)(2,1)S(1)} %constant_dynamic-update-slice_fusion.2.refs_0_), channel_id=1, source_target_pairs={{0,1},{1,0},{2,3},{3,2},{4,5},{5,4},{6,7},{7,6},{8,9},{9,8},{10,11... | collective-permute-start | bytes 1769480 | tf_op jit(solution)/shard_map/ppermute | solution.py:22
  67.7 16.8 %copy-start.1 = (bf16[576,512]{1,0:T(8,128)(2,1)}, bf16[576,512]{1,0:T(8,128)(2,1)S(1)}, u32[]{:S(2)}) copy-start(bf16[576,512]{1,0:T(8,128)(2,1)S(1)} %collective-permute-done.6.refs_3_) | copy-start | bytes 1769476
  67.7 14.9 %collective-permute-start.10 = (bf16[576,512]{1,0:T(8,128)(2,1)S(1)}, bf16[576,512]{1,0:T(8,128)(2,1)S(1)}, u32[]{:S(2)}, u32[]{:S(2)}) collective-permute-start(bf16[576,512]{1,0:T(8,128)(2,1)S(1)} %collective-permute-done.6.refs_3_), channel_id=1, source_target_pairs={{0,1},{1,0},{2,3},{3,2},{4,5},{5,4},{6,7},{7,6},{8,9},{9,8},{10,11... | collective-permute-start | bytes 1769480 | tf_op jit(solution)/shard_map/ppermute | solution.py:22
  78.2 6.3 %copy-start.2 = (bf16[576,512]{1,0:T(8,128)(2,1)}, bf16[576,512]{1,0:T(8,128)(2,1)S(1)}, u32[]{:S(2)}) copy-start(bf16[576,512]{1,0:T(8,128)(2,1)S(1)} %collective-permute-done.4.refs_1_) | copy-start | bytes 1769476
  78.2 5.4 %collective-permute-start.8 = (bf16[576,512]{1,0:T(8,128)(2,1)S(1)}, bf16[576,512]{1,0:T(8,128)(2,1)}, u32[]{:S(2)}, u32[]{:S(2)}) collective-permute-start(bf16[576,512]{1,0:T(8,128)(2,1)S(1)} %collective-permute-done.4.refs_1_), channel_id=1, source_target_pairs={{0,1},{1,0},{2,3},{3,2},{4,5},{5,4},{6,7},{7,6},{8,9},{9,8},{10,11... | collective-permute-start | bytes 1769480 | tf_op jit(solution)/shard_map/ppermute | solution.py:22
  81.8 2.6 %copy-start.3 = (bf16[576,512]{1,0:T(8,128)(2,1)}, bf16[576,512]{1,0:T(8,128)(2,1)S(1)}, u32[]{:S(2)}) copy-start(bf16[576,512]{1,0:T(8,128)(2,1)S(1)} %collective-permute-done.5.refs_2_) | copy-start | bytes 1769476
  81.8 2.6 %collective-permute-start.9 = (bf16[576,512]{1,0:T(8,128)(2,1)S(1)}, bf16[576,512]{1,0:T(8,128)(2,1)}, u32[]{:S(2)}, u32[]{:S(2)}) collective-permute-start(bf16[576,512]{1,0:T(8,128)(2,1)S(1)} %collective-permute-done.5.refs_2_), channel_id=1, source_target_pairs={{0,1},{1,0},{2,3},{3,2},{4,5},{5,4},{6,7},{7,6},{8,9},{9,8},{10,11... | collective-permute-start | bytes 1769480 | tf_op jit(solution)/shard_map/ppermute | solution.py:22
  82.6 1.8 copy-start.4
  82.7 1.8 copy-start.5
  90.1 25.9 %copy-start.19 = (f32[1024,16]{0,1:T(8,128)S(1)}, f32[1024,16]{0,1:T(8,128)}, u32[]{:S(2)}) copy-start(f32[1024,16]{0,1:T(8,128)} %param.19) | copy-start | bytes 196612
  103.8 2.6 %collective-permute-start.14 = (f32[64,544]{1,0:T(8,128)}, f32[64,544]{1,0:T(8,128)S(1)}, u32[]{:S(2)}, u32[]{:S(2)}) collective-permute-start(f32[64,544]{1,0:T(8,128)} %get-tuple-element.26), channel_id=1, source_target_pairs={{0,1},{1,0},{2,3},{3,2},{4,5},{5,4},{6,7},{7,6},{8,9},{9,8},{10,11... | collective-permute-start | bytes 417800 | tf_op jit(solution)/shard_map/ppermute | solution.py:22
  107.3 6.9 %collective-permute-start.15 = (bf16[64,544]{1,0:T(8,128)(2,1)S(1)}, bf16[64,544]{1,0:T(8,128)(2,1)S(1)}, u32[]{:S(2)}, u32[]{:S(2)}) collective-permute-start(bf16[64,544]{1,0:T(8,128)(2,1)S(1)} %get-tuple-element.43), channel_id=1, source_target_pairs={{0,2},{2,4},{4,6},{6,0},{1,3},{3,5},{5,7},{7,1},{8,10},{10,12},{12... | collective-permute-start | bytes 208904 | tf_op jit(solution)/shard_map/ppermute | solution.py:22
  107.4 6.8 %collective-permute-start.16 = (bf16[64,544]{1,0:T(8,128)(2,1)S(1)}, bf16[64,544]{1,0:T(8,128)(2,1)S(1)}, u32[]{:S(2)}, u32[]{:S(2)}) collective-permute-start(bf16[64,544]{1,0:T(8,128)(2,1)S(1)} %get-tuple-element.43), channel_id=1, source_target_pairs={{0,4},{2,6},{4,0},{6,2},{1,5},{3,7},{5,1},{7,3},{8,12},{10,14},{12... | collective-permute-start | bytes 208904 | tf_op jit(solution)/shard_map/ppermute | solution.py:22
  109.2 5.2 %collective-permute-start.17 = (bf16[64,544]{1,0:T(8,128)(2,1)S(1)}, bf16[64,544]{1,0:T(8,128)(2,1)S(1)}, u32[]{:S(2)}, u32[]{:S(2)}) collective-permute-start(bf16[64,544]{1,0:T(8,128)(2,1)S(1)} %get-tuple-element.43), channel_id=1, source_target_pairs={{0,6},{2,0},{4,2},{6,4},{1,7},{3,1},{5,3},{7,5},{8,14},{10,8},{12,... | collective-permute-start | bytes 208904 | tf_op jit(solution)/shard_map/ppermute | solution.py:22
  114.4 2.6 %copy-start.6 = (f32[64,544]{1,0:T(8,128)}, f32[64,544]{1,0:T(8,128)S(1)}, u32[]{:S(2)}) copy-start(f32[64,544]{1,0:T(8,128)S(1)} %convert_add_fusion.mine_ref) | copy-start | bytes 417796
  114.4 2.6 %collective-permute-start.18 = (f32[64,544]{1,0:T(8,128)S(1)}, f32[64,544]{1,0:T(8,128)S(1)}, u32[]{:S(2)}, u32[]{:S(2)}) collective-permute-start(f32[64,544]{1,0:T(8,128)S(1)} %convert_add_fusion.mine_ref), channel_id=1, source_target_pairs={{0,1},{1,0},{2,3},{3,2},{4,5},{5,4},{6,7},{7,6},{8,9},{9,8},{10,11... | collective-permute-start | bytes 417800 | tf_op jit(solution)/shard_map/ppermute | solution.py:22
  147.1 16.7 %all-to-all-start.2 = ((bf16[4,18,8,128]{3,2,1,0:T(8,128)(2,1)}), bf16[4,18,8,128]{3,2,1,0:T(8,128)(2,1)S(1)}, u32[]{:S(2)}, u32[]{:S(2)}) async-start(bf16[4,18,8,128]{3,2,1,0:T(8,128)(2,1)} %get-tuple-element.30), calls=%async_computation.2 | async-start | bytes 294912 | tf_op jit(solution)/shard_map/all_to_all | solution.py:428
  155.6 4.3 %collective-permute-start.19 = (bf16[128,256]{1,0:T(8,128)(2,1)}, bf16[128,256]{1,0:T(8,128)(2,1)S(1)}, u32[]{:S(2)}, u32[]{:S(2)}) collective-permute-start(bf16[128,256]{1,0:T(8,128)(2,1)} %get-tuple-element.34), channel_id=1, source_target_pairs={{0,192},{64,0},{128,64},{192,128},{1,193},{65,1},{129,65},{193,129... | collective-permute-start | bytes 196616 | tf_op jit(solution)/shard_map/ppermute | solution.py:22
  158.3 4.9 %collective-permute-start.20 = (bf16[128,256]{1,0:T(8,128)(2,1)}, bf16[128,256]{1,0:T(8,128)(2,1)S(1)}, u32[]{:S(2)}, u32[]{:S(2)}) collective-permute-start(bf16[128,256]{1,0:T(8,128)(2,1)} %get-tuple-element.35), channel_id=1, source_target_pairs={{0,128},{64,192},{128,0},{192,64},{1,129},{65,193},{129,1},{193,65... | collective-permute-start | bytes 196616 | tf_op jit(solution)/shard_map/ppermute | solution.py:22
  158.8 5.0 %collective-permute-start.21 = (bf16[128,256]{1,0:T(8,128)(2,1)}, bf16[128,256]{1,0:T(8,128)(2,1)S(1)}, u32[]{:S(2)}, u32[]{:S(2)}) collective-permute-start(bf16[128,256]{1,0:T(8,128)(2,1)} %get-tuple-element.36), channel_id=1, source_target_pairs={{0,64},{64,128},{128,192},{192,0},{1,65},{65,129},{129,193},{193,1... | collective-permute-start | bytes 196616 | tf_op jit(solution)/shard_map/ppermute | solution.py:22
  159.9 3.9 %copy-start.16 = (bf16[128,256]{1,0:T(8,128)(2,1)}, bf16[128,256]{1,0:T(8,128)(2,1)S(1)}, u32[]{:S(2)}) copy-start(bf16[128,256]{1,0:T(8,128)(2,1)S(1)} %collective-permute-done.19.refs_1_) | copy-start | bytes 196612
  169.7 8.4 %collective-permute-start.22 = (bf16[128,1024]{1,0:T(8,128)(2,1)}, bf16[128,1024]{1,0:T(8,128)(2,1)S(1)}, u32[]{:S(2)}, u32[]{:S(2)}) collective-permute-start(bf16[128,1024]{1,0:T(8,128)(2,1)} %shard_map.114), channel_id=1, source_target_pairs={{0,0},{2,64},{4,128},{6,192},{64,2},{66,66},{68,130},{70,194},{128... | collective-permute-start | bytes 786440 | tf_op jit(solution)/shard_map/ppermute | solution.py:446
  171.3 15.9 %collective-permute-start.23 = (bf16[128,1024]{1,0:T(8,128)(2,1)}, bf16[128,1024]{1,0:T(8,128)(2,1)S(1)}, u32[]{:S(2)}, u32[]{:S(2)}) collective-permute-start(bf16[128,1024]{1,0:T(8,128)(2,1)} %shard_map.114), channel_id=1, source_target_pairs={{0,2},{2,66},{4,130},{6,194},{64,4},{66,68},{68,132},{70,196},{128... | collective-permute-start | bytes 786440 | tf_op jit(solution)/shard_map/ppermute | solution.py:446
  172.3 14.9 %collective-permute-start.24 = (bf16[128,1024]{1,0:T(8,128)(2,1)}, bf16[128,1024]{1,0:T(8,128)(2,1)S(1)}, u32[]{:S(2)}, u32[]{:S(2)}) collective-permute-start(bf16[128,1024]{1,0:T(8,128)(2,1)} %shard_map.114), channel_id=1, source_target_pairs={{0,4},{2,68},{4,132},{6,196},{64,6},{66,70},{68,134},{70,198},{128... | collective-permute-start | bytes 786440 | tf_op jit(solution)/shard_map/ppermute | solution.py:446
  175.4 12.1 %collective-permute-start.25 = (bf16[128,1024]{1,0:T(8,128)(2,1)}, bf16[128,1024]{1,0:T(8,128)(2,1)S(1)}, u32[]{:S(2)}, u32[]{:S(2)}) collective-permute-start(bf16[128,1024]{1,0:T(8,128)(2,1)} %shard_map.114), channel_id=1, source_target_pairs={{0,6},{2,70},{4,134},{6,198},{64,0},{66,64},{68,128},{70,192},{128... | collective-permute-start | bytes 786440 | tf_op jit(solution)/shard_map/ppermute | solution.py:446
  178.1 9.5 %copy-start.11 = (bf16[128,1024]{1,0:T(8,128)(2,1)}, bf16[128,1024]{1,0:T(8,128)(2,1)S(1)}, u32[]{:S(2)}) copy-start(bf16[128,1024]{1,0:T(8,128)(2,1)S(1)} %collective-permute-done.22.refs_0_) | copy-start | bytes 786436
  192.7 4.3 %collective-permute-start.27 = (bf16[4,128,512]{2,1,0:T(8,128)(2,1)}, bf16[4,128,512]{2,1,0:T(8,128)(2,1)S(1)}, u32[]{:S(2)}, u32[]{:S(2)}) collective-permute-start(bf16[4,128,512]{2,1,0:T(8,128)(2,1)} %get-tuple-element.38), channel_id=1, source_target_pairs={{0,1},{1,0},{2,3},{3,2},{4,5},{5,4},{6,7},{7,6},{8,9},{9,8},{10,11... | collective-permute-start | bytes 1572872 | tf_op jit(solution)/shard_map/ppermute | solution.py:22
  197.0 0.8 copy-start.9
  199.9 7.7 %collective-permute-start.28 = (bf16[128,512]{1,0:T(8,128)(2,1)}, bf16[128,512]{1,0:T(8,128)(2,1)S(1)}, u32[]{:S(2)}, u32[]{:S(2)}) collective-permute-start(bf16[128,512]{1,0:T(8,128)(2,1)} %get-tuple-element.40), channel_id=1, source_target_pairs={{0,64},{64,128},{128,192},{192,0},{1,65},{65,129},{129,193},{193,1... | collective-permute-start | bytes 393224 | tf_op jit(solution)/shard_map/ppermute | solution.py:22
  202.3 9.0 %collective-permute-start.29 = (bf16[128,512]{1,0:T(8,128)(2,1)}, bf16[128,512]{1,0:T(8,128)(2,1)S(1)}, u32[]{:S(2)}, u32[]{:S(2)}) collective-permute-start(bf16[128,512]{1,0:T(8,128)(2,1)} %get-tuple-element.41), channel_id=1, source_target_pairs={{0,128},{64,192},{128,0},{192,64},{1,129},{65,193},{129,1},{193,65... | collective-permute-start | bytes 393224 | tf_op jit(solution)/shard_map/ppermute | solution.py:22
  205.1 6.2 %collective-permute-start.30 = (bf16[128,512]{1,0:T(8,128)(2,1)}, bf16[128,512]{1,0:T(8,128)(2,1)S(1)}, u32[]{:S(2)}, u32[]{:S(2)}) collective-permute-start(bf16[128,512]{1,0:T(8,128)(2,1)} %get-tuple-element.42), channel_id=1, source_target_pairs={{0,192},{64,0},{128,64},{192,128},{1,193},{65,1},{129,65},{193,129... | collective-permute-start | bytes 393224 | tf_op jit(solution)/shard_map/ppermute | solution.py:22
  (8 other events, 5.6 us)
Sparse Core Ops, SparseCore 0:
  17.7 40.4 all-gather.3
  60.0 39.4 all-gather.5
  101.2 50.5 all-gather.7
